TPU v7x, 8 devices: a whole 2x2x1 slice. The times are simulated.
8 devices in a mesh: model: 2 (over z, y), data: 4 (over x, core).
Axes of the slice: x: 2, y: 2, z: 1, core: 2. Of those that a mesh axis runs over, the one named last changes fastest.
Arguments:
- act_in: bfloat16 [32768, 1280], P('data')
- grad_out: bfloat16 [32768, 1280], P('data')
- w_up: bfloat16 [2, 1280, 5120], P(None, None, 'model')
- w_down: bfloat16 [2, 5120, 1280], P(None, 'model')
- master_up: float32 [2, 1280, 5120], P(None, 'data', 'model')
- master_down: float32 [2, 5120, 1280], P(None, ('model', 'data'))
- mom_up: float32 [2, 1280, 5120], P(None, 'data', 'model')
- mom_down: float32 [2, 5120, 1280], P(None, ('model', 'data'))
- var_up: float32 [2, 1280, 5120], P(None, 'data', 'model')
- var_down: float32 [2, 5120, 1280], P(None, ('model', 'data'))
- learn_rate: float32 [1], replicated
- clip_norm: float32 [1], replicated
Outputs:
- output 1: bfloat16 [2, 1280, 5120], P(None, None, 'model')
- output 2: bfloat16 [2, 5120, 1280], P(None, 'model')
- output 3: float32 [2, 1280, 5120], P(None, 'data', 'model')
- output 4: float32 [2, 5120, 1280], P(None, ('model', 'data'))
- output 5: float32 [2, 1280, 5120], P(None, 'data', 'model')
- output 6: float32 [2, 5120, 1280], P(None, ('model', 'data'))
- output 7: float32 [2, 1280, 5120], P(None, 'data', 'model')
- output 8: float32 [2, 5120, 1280], P(None, ('model', 'data'))
- output 9: float32 [1], replicated
All inputs are finite; a program needn't handle non-finite values.
Results may differ from a plain program's by a relative error of at most 0.00147533.
Values are sent between devices in bfloat16 or wider.
A program may use at most 1 GiB of HBM per device.

v0:
```python
import jax
import jax.numpy as jnp
from jax import lax
from jax.sharding import PartitionSpec as P

STEP = 10
BETA_ONE = 0.9
BETA_TWO = 0.95
ADAM_EPS = 1e-8
NORM_EPS = 1e-6


def gelu_fwd(z_low):
    return jax.nn.gelu(z_low.astype(jnp.float32)).astype(jnp.bfloat16)


def gelu_back(z_low, grad_low):
    _, back_fn = jax.vjp(jax.nn.gelu, z_low.astype(jnp.float32))
    return back_fn(grad_low.astype(jnp.float32))[0].astype(jnp.bfloat16)


def adam_update(master_arr, mom_arr, var_arr, grad_arr, clip_scale, lr_val):
    scaled = clip_scale * grad_arr
    new_mom = BETA_ONE * mom_arr + (1.0 - BETA_ONE) * scaled
    new_var = BETA_TWO * var_arr + (1.0 - BETA_TWO) * scaled * scaled
    mom_hat = new_mom / (1.0 - BETA_ONE ** STEP)
    var_hat = new_var / (1.0 - BETA_TWO ** STEP)
    new_master = master_arr - lr_val * mom_hat / (jnp.sqrt(var_hat) + ADAM_EPS)
    return new_master, new_mom, new_var


def local_grads(act_in, grad_out, w_up, w_down):
    z_one = jnp.dot(act_in, w_up[0], preferred_element_type=jnp.float32).astype(jnp.bfloat16)
    act_one = gelu_fwd(z_one)
    hid_part = jnp.dot(act_one, w_down[0], preferred_element_type=jnp.float32)
    hid_two = lax.psum(hid_part, "model").astype(jnp.bfloat16)
    z_two = jnp.dot(hid_two, w_up[1], preferred_element_type=jnp.float32).astype(jnp.bfloat16)
    act_two = gelu_fwd(z_two)
    grad_w4 = jnp.einsum("bf,bd->fd", act_two, grad_out, preferred_element_type=jnp.float32)
    dact_two = jnp.einsum("bd,fd->bf", grad_out, w_down[1], preferred_element_type=jnp.float32).astype(jnp.bfloat16)
    dz_two = gelu_back(z_two, dact_two)
    grad_w3 = jnp.einsum("bd,bf->df", hid_two, dz_two, preferred_element_type=jnp.float32)
    dhid_part = jnp.einsum("bf,df->bd", dz_two, w_up[1], preferred_element_type=jnp.float32)
    dhid_two = lax.psum(dhid_part, "model").astype(jnp.bfloat16)
    grad_w2 = jnp.einsum("bf,bd->fd", act_one, dhid_two, preferred_element_type=jnp.float32)
    dact_one = jnp.einsum("bd,fd->bf", dhid_two, w_down[0], preferred_element_type=jnp.float32).astype(jnp.bfloat16)
    dz_one = gelu_back(z_one, dact_one)
    grad_w1 = jnp.einsum("bd,bf->df", act_in, dz_one, preferred_element_type=jnp.float32)
    return grad_w1, grad_w3, grad_w2, grad_w4


def solution(mesh):
    data_size = mesh.shape["data"]
    spec_rows = P("data", None)
    spec_wup = P(None, None, "model")
    spec_wdown = P(None, "model", None)
    spec_sup = P(None, "data", "model")
    spec_sdown = P(None, ("model", "data"), None)
    spec_scalar = P(None)

    def local_step(act_in, grad_out, w_up, w_down, master_up, master_down, mom_up, mom_down, var_up, var_down, learn_rate, clip_norm):
        grad_w1, grad_w3, grad_w2, grad_w4 = local_grads(act_in, grad_out, w_up, w_down)
        shard_w4 = lax.psum_scatter(grad_w4, "data", scatter_dimension=0, tiled=True)
        shard_w3 = lax.psum_scatter(grad_w3, "data", scatter_dimension=0, tiled=True)
        shard_w2 = lax.psum_scatter(grad_w2, "data", scatter_dimension=0, tiled=True)
        shard_w1 = lax.psum_scatter(grad_w1, "data", scatter_dimension=0, tiled=True)
        grad_up = jnp.stack([shard_w1, shard_w3]) / data_size
        grad_down = jnp.stack([shard_w2, shard_w4]) / data_size
        sq_local = jnp.sum(grad_up * grad_up) + jnp.sum(grad_down * grad_down)
        norm_val = jnp.sqrt(lax.psum(sq_local, ("model", "data")))
        clip_scale = jnp.minimum(1.0, clip_norm[0] / (norm_val + NORM_EPS))
        lr_val = learn_rate[0]
        new_master_up, new_mom_up, new_var_up = adam_update(master_up, mom_up, var_up, grad_up, clip_scale, lr_val)
        new_master_down, new_mom_down, new_var_down = adam_update(master_down, mom_down, var_down, grad_down, clip_scale, lr_val)
        new_w_up = lax.all_gather(new_master_up.astype(jnp.bfloat16), "data", axis=1, tiled=True)
        new_w_down = lax.all_gather(new_master_down.astype(jnp.bfloat16), "data", axis=1, tiled=True)
        return (new_w_up, new_w_down, new_master_up, new_master_down, new_mom_up, new_mom_down, new_var_up, new_var_down, norm_val.reshape(1))

    return jax.shard_map(local_step, mesh=mesh, in_specs=(spec_rows, spec_rows, spec_wup, spec_wdown, spec_sup, spec_sdown, spec_sup, spec_sdown, spec_sup, spec_sdown, spec_scalar, spec_scalar), out_specs=(spec_wup, spec_wdown, spec_sup, spec_sdown, spec_sup, spec_sdown, spec_sup, spec_sdown, spec_scalar), check_vma=False)
```

profile of v0, /device:TPU:0, one launch (start us, length us, event | category | flops | bytes accessed | tf_op | source)
XLA Modules:
  0.0 3023.1 jit_solution(29955919311897178)
XLA Ops:
  7.2 0.0 reduce-scatter.15.cloned.1.call-start
  7.2 62.4 %convolution_convert_fusion.2 = bf16[8192,2560]{1,0:T(8,128)(2,1)} fusion(bf16[8192,1280]{1,0:T(8,128)(2,1)} %param.12, bf16[2,1280,2560]{2,1,0:T(8,128)(2,1)} %param.14), kind=kOutput, calls=%fused_computation.36 | convolution fusion | flops 53708062720 | bytes 69468160 | tf_op jit(solution)/shard_map/dot_general | solution.py:33
  69.6 82.3 %fusion.40 = f32[8192,1280]{1,0:T(8,128)} fusion(bf16[2,2560,1280]{2,1,0:T(8,128)(2,1)} %param.15, bf16[8192,2560]{1,0:T(8,128)(2,1)} %convolution_convert_fusion.2), kind=kOutput, calls=%fused_computation.60 | convolution fusion | flops 53896806400 | bytes 90439680 | tf_op jit(solution)/shard_map/dot_general | solution.py:35
  151.9 949.7 %all-reduce.2 = bf16[8192,1280]{1,0:T(8,128)(2,1)} all-reduce(f32[8192,1280]{1,0:T(8,128)} %fusion.40), channel_id=1, replica_groups=mesh['model'=2,'data'=4] {'model'}, use_global_device_ids=true, to_apply=%region_0.0 | all-reduce | flops 10485760 | bytes 62914560 | tf_op jit(solution)/shard_map/psum | solution.py:36
  1101.7 62.6 %convolution_convert_fusion.1 = bf16[8192,2560]{1,0:T(8,128)(2,1)} fusion(bf16[8192,1280]{1,0:T(8,128)(2,1)} %all-reduce.2, bf16[2,1280,2560]{2,1,0:T(8,128)(2,1)} %param.14), kind=kOutput, calls=%fused_computation.35 | convolution fusion | flops 53708062720 | bytes 69468160 | tf_op jit(solution)/shard_map/dot_general | solution.py:37
  1164.3 109.6 %fusion.4 = bf16[8192,2560]{1,0:T(8,128)(2,1)} fusion(bf16[8192,2560]{1,0:T(8,128)(2,1)} %convolution_convert_fusion.1, bf16[8192,1280]{1,0:T(8,128)(2,1)} %param.13, bf16[2,2560,1280]{2,1,0:T(8,128)(2,1)} %param.15), kind=kOutput, calls=%fused_computation.16 | convolution fusion | flops 54169436160 | bytes 111411200 | tf_op jit(solution)/shard_map/bd,fd->bf/dot_general | solution.py:40
  1273.9 63.5 %fusion.67 = f32[1280,2560]{1,0:T(8,128)} fusion(bf16[8192,1280]{1,0:T(8,128)(2,1)} %all-reduce.2, bf16[8192,2560]{1,0:T(8,128)(2,1)} %fusion.4), kind=kOutput, calls=%fused_computation.85 | convolution fusion | flops 53687091200 | bytes 76021760
  1337.4 0.0 reduce-scatter.15.cloned.1.call-update
  1337.4 0.0 reduce-scatter.11.cloned.1.call-start
  1337.5 73.4 %fusion.22 = f32[2560,1280]{1,0:T(8,128)} fusion(bf16[8192,1280]{1,0:T(8,128)(2,1)} %param.13, bf16[8192,2560]{1,0:T(8,128)(2,1)} %convolution_convert_fusion.1), kind=kOutput, calls=%fused_computation.38 | convolution fusion | flops 53896806400 | bytes 76021760 | tf_op jit(solution)/shard_map/bf,bd->fd/dot_general | solution.py:39
  1410.9 0.0 reduce-scatter.11.cloned.1.call-update
  1410.9 0.0 reduce-scatter.9.cloned.1.call-start
  1411.0 64.0 %fusion.35 = f32[8192,1280]{1,0:T(8,128)} fusion(bf16[8192,2560]{1,0:T(8,128)(2,1)} %fusion.4, bf16[2,1280,2560]{2,1,0:T(8,128)(2,1)} %param.14), kind=kOutput, calls=%fused_computation.56 | convolution fusion | flops 53687091200 | bytes 90439680 | tf_op jit(solution)/shard_map/bf,df->bd/dot_general | solution.py:43
  1475.0 938.9 %all-reduce.3 = bf16[8192,1280]{1,0:T(8,128)(2,1)} all-reduce(f32[8192,1280]{1,0:T(8,128)} %fusion.35), channel_id=1, replica_groups=mesh['model'=2,'data'=4] {'model'}, use_global_device_ids=true, to_apply=%region_1.0 | all-reduce | flops 10485760 | bytes 62914560 | tf_op jit(solution)/shard_map/psum | solution.py:44
  2413.9 73.4 %fusion.26 = f32[2560,1280]{1,0:T(8,128)} fusion(bf16[8192,1280]{1,0:T(8,128)(2,1)} %all-reduce.3, bf16[8192,2560]{1,0:T(8,128)(2,1)} %convolution_convert_fusion.2), kind=kOutput, calls=%fused_computation.42 | convolution fusion | flops 53896806400 | bytes 76021760 | tf_op jit(solution)/shard_map/bf,bd->fd/dot_general | solution.py:45
  2487.3 0.0 reduce-scatter.9.cloned.1.call-update
  2487.3 0.0 reduce-scatter.13.cloned.1.call-start
  2487.3 110.0 %fusion.7.clone.6 = bf16[8192,2560]{1,0:T(8,128)(2,1)} fusion(bf16[8192,2560]{1,0:T(8,128)(2,1)} %convolution_convert_fusion.2, bf16[8192,1280]{1,0:T(8,128)(2,1)} %all-reduce.3, bf16[2,2560,1280]{2,1,0:T(8,128)(2,1)} %param.15), kind=kOutput, calls=%fused_computation.19.clone.clone.clone.clone.clone.1 | convolution fusion | flops 54169436160 | bytes 111411200 | tf_op jit(solution)/shard_map/bd,fd->bf/dot_general | solution.py:46
  2597.4 63.5 %fusion.25 = f32[1280,2560]{0,1:T(8,128)} fusion(bf16[8192,1280]{1,0:T(8,128)(2,1)} %param.12, bf16[8192,2560]{1,0:T(8,128)(2,1)} %fusion.7.clone.6), kind=kOutput, calls=%fused_computation.40 | convolution fusion | flops 53687091200 | bytes 76021760 | tf_op jit(solution)/shard_map/bd,bf->df/dot_general | solution.py:48
  2660.9 14.0 copy.39
  2674.9 0.0 reduce-scatter.13.cloned.1.call-update
  2674.9 0.0 all-gather.3.cloned.1.call-start
  2676.2 8.5 copy.32
  2684.7 8.5 copy.29
  2693.3 8.5 copy.31
  2701.8 0.0 reduce-scatter.15.cloned.1.call-done
  2701.8 5.1 copy.42
  2706.8 0.0 reduce-scatter.11.cloned.1.call-done
  2706.8 0.0 reduce-scatter.9.cloned.1.call-done
  2706.8 5.2 multiply_reduce_fusion.1
  2712.1 55.9 %reduce-scatter.13.cloned.1.call-done = f32[320,2560]{1,0:T(8,128)} async-done(((f32[1280,2560]{1,0:T(8,128)}), f32[320,2560]{1,0:T(8,128)}) %reduce-scatter.13.cloned.1.call-update) | async-done | bytes 3276816
  2768.0 5.1 copy.40
  2773.1 4.9 multiply_reduce_fusion
  2779.3 22.5 psum.23
  2802.5 0.0 copy-start
  2802.5 21.7 fusion.65
  2824.2 10.5 copy.33
  2834.7 0.0 all-gather.3.cloned.1.call-update
  2834.8 0.0 all-gather.5.cloned.1.call-start
  2834.8 0.0 copy-done
  2834.8 14.4 fusion.63
  2849.3 0.0 all-gather.5.cloned.1.call-update
  2849.3 8.6 copy.35
  2857.9 8.6 copy.36
  2866.4 8.6 copy.37
  2875.0 44.8 %all-gather.3.cloned.1.call-done = bf16[2,1280,2560]{2,0,1:T(2,128)(2,1)} async-done(((bf16[2,320,2560]{2,0,1:T(2,128)(2,1)}), bf16[2,1280,2560]{2,0,1:T(2,128)(2,1)}) %all-gather.3.cloned.1.call-update) | async-done | bytes 13107216 | tf_op jit(solution)/shard_map/all_gather | solution.py:75
  2919.8 12.1 copy.34
  2931.9 72.3 %all-gather.5.cloned.1.call-done = bf16[2,2560,1280]{2,1,0:T(8,128)(2,1)} async-done(((bf16[2,640,1280]{2,1,0:T(8,128)(2,1)}), bf16[2,2560,1280]{2,1,0:T(8,128)(2,1)}) %all-gather.5.cloned.1.call-update) | async-done | bytes 13107216 | tf_op jit(solution)/shard_map/all_gather | solution.py:76
  3004.2 10.7 copy.50
Async XLA Ops:
  7.2 2694.6 %reduce-scatter.15.cloned.1.call-start = ((), (), s32[]{:S(2)}) async-start(), calls=%async_computation.9 | async-start | bytes 16384000
  1337.4 1369.4 %reduce-scatter.11.cloned.1.call-start = ((), (), s32[]{:S(2)}) async-start(), calls=%async_computation.5 | async-start | bytes 16384000 | tf_op jit(solution)/shard_map/reduce_scatter | solution.py:63
  1410.9 1295.9 %reduce-scatter.9.cloned.1.call-start = ((), (), s32[]{:S(2)}) async-start(), calls=%async_computation.4 | async-start | bytes 16384000 | tf_op jit(solution)/shard_map/reduce_scatter | solution.py:65
  2487.3 280.7 %reduce-scatter.13.cloned.1.call-start = ((), (), s32[]{:S(2)}) async-start(), calls=%async_computation.8 | async-start | bytes 16384000
  2674.9 244.9 %all-gather.3.cloned.1.call-start = ((), (), s32[]{:S(2)}) async-start(), calls=%async_computation.6 | async-start | bytes 16384000 | tf_op jit(solution)/shard_map/all_gather | solution.py:75
  2802.5 32.3 %copy-start = (f32[640,1280]{1,0:T(8,128)S(1)}, f32[640,1280]{1,0:T(8,128)}, u32[]{:S(2)}) copy-start(f32[640,1280]{1,0:T(8,128)} %reduce-scatter.11.cloned.1.call-done) | copy-start | bytes 9830404
  2834.8 169.4 %all-gather.5.cloned.1.call-start = ((), (), s32[]{:S(2)}) async-start(), calls=%async_computation.7 | async-start | bytes 16384000 | tf_op jit(solution)/shard_map/all_gather | solution.py:76
Sparse Core Ops, SparseCore 0:
  1337.6 93.8 reduce-scatter.14
  1434.1 93.6 reduce-scatter.10
  2487.4 92.9 reduce-scatter.8
  2675.0 92.9 reduce-scatter.12
  2834.9 84.8 all-gather.2
  2921.2 82.9 all-gather.4
where the time goes:
time: 3030 us; the launch traced here: 3020 us
  blocking collectives  1910 us (63%)
  matrix products  765 us (25%)
  waiting for transfers between devices  173 us (6%)
  local copies, waits for them, and re-layouts  109 us (4%)
  other arithmetic  46.3 us (2%)
    psum x1, blocking collectives, local_grads(): hid_two = lax.psum(hid_part, 'model').astype(jnp.bfloat16)  950 us
    psum x1, blocking collectives, local_grads(): dhid_two = lax.psum(dhid_part, 'model').astype(jnp.bfloat16)  939 us
    dot_general x1, matrix products, local_grads(): jnp.einsum('bd,fd->bf', dhid_two, w_down[0], preferred_element_type=jnp.f...  110 us
    dot_general x1, matrix products, local_grads(): jnp.einsum('bd,fd->bf', grad_out, w_down[1], preferred_element_type=jnp.f...  110 us
    unnamed x13, local copies, waits for them, and re-layouts  98.2 us
    dot_general x1, matrix products, local_grads(): hid_part = jnp.dot(act_one, w_down[0], preferred_element_type=jnp.float32)  82.3 us
    dot_general x1, matrix products, local_grads(): jnp.einsum('bf,bd->fd', act_two, grad_out, preferred_element_type=jnp.flo...  73.4 us
    dot_general x1, matrix products, local_grads(): jnp.einsum('bf,bd->fd', act_one, dhid_two, preferred_element_type=jnp.flo...  73.4 us
  transfers between devices with their start and end apart: 6, of which 3 were waited for; matrix products, arithmetic and copies ran while one was open for 16% of the time, Pallas kernels for 0%

commit v1 on v0

v1 whole, which is shorter than its diff:
```python
import functools

import jax
import jax.numpy as jnp
from jax import lax
from jax.experimental import pallas as pl
from jax.experimental.pallas import tpu as pltpu
from jax.sharding import PartitionSpec as P

STEP = 10
BETA_ONE = 0.9
BETA_TWO = 0.95
ADAM_EPS = 1e-8
NORM_EPS = 1e-6
MESH = pl.DeviceIdType.MESH
F32 = jnp.float32
BF16 = jnp.bfloat16
GELU_ONE = 0.7978845608028654
GELU_TWO = GELU_ONE * 0.044715
IS_UP = (False, True, False, True)
PIECES = (("s", 0), ("s", 1), ("s", 2), ("m", 0), ("s", 3), ("m", 1), ("m", 2), ("m", 3))
SUBS = 2


def adam_update(master_arr, mom_arr, var_arr, grad_arr, clip_scale, lr_val):
    scaled = clip_scale * grad_arr
    new_mom = BETA_ONE * mom_arr + (1.0 - BETA_ONE) * scaled
    new_var = BETA_TWO * var_arr + (1.0 - BETA_TWO) * scaled * scaled
    mom_hat = new_mom / (1.0 - BETA_ONE ** STEP)
    var_hat = new_var / (1.0 - BETA_TWO ** STEP)
    new_master = master_arr - lr_val * mom_hat / (jnp.sqrt(var_hat) + ADAM_EPS)
    return new_master, new_mom, new_var


def gelu_half(z):
    return 0.5 + 0.5 * jnp.tanh(z * (GELU_ONE + GELU_TWO * (z * z)))


def gelu_slope(z):
    sig = gelu_half(z)
    wide = z * (2.0 * GELU_ONE + (6.0 * GELU_TWO) * (z * z))
    return sig * (1.0 + (1.0 - sig) * wide)


def dot_nn(a, b):
    return jnp.dot(a, b, preferred_element_type=F32)


def dot_nt(a, b):
    return lax.dot_general(a, b, (((1,), (1,)), ((), ())), preferred_element_type=F32)


def dot_tn(a, b):
    return lax.dot_general(a, b, (((0,), (0,)), ((), ())), preferred_element_type=F32)


def grad_kernel(
    rows, bm, nc,
    x, dy, wu, wd, zeros,
    gfin, gsib, nrm, wou, wod, z1, a1, z3, a3, q3, q1, hbuf, hpart, pss, psm, rc, rx, ry, x3,
    wb, ring, gacc, outs, res, gs, side, ss, nbuf,
    s_x, s_w, s_ring, s_out, s_gacc, s_ps, s_res, s_gs, s_side,
    w_snd, w_rcv, g_snd, g_rcv, f_snd, f_rcv, n_snd, n_rcv,
):
    yy = lax.axis_index("model")
    dd = lax.axis_index("data")
    xx = dd // 2
    cc = dd % 2
    me = yy * 4 + dd
    d_sib = 2 * xx + (1 - cc)
    d_far = 2 * (1 - xx) + cc
    d_diag = 2 * (1 - xx) + (1 - cc)
    sib, xnb, ynb = (yy, d_sib), (yy, d_far), (1 - yy, dd)
    dim = x.shape[1]
    half = dim // 2
    quart = dim // 4
    nr = rows // bm
    kr = rows // 2
    row0 = yy * rows
    chunks = [slice(n, n + nc) for n in range(0, dim, nc)]

    def aligned(v, m):
        return pl.multiple_of(v, m)

    def local(src, dst, sem):
        return pltpu.make_async_copy(src, dst, sem)

    def remote(src, dst, snd, rcv, dev):
        return pltpu.make_async_remote_copy(
            src_ref=src, dst_ref=dst, send_sem=snd, recv_sem=rcv, device_id=dev, device_id_type=MESH
        )

    barrier = pltpu.get_barrier_semaphore()
    for o in range(1, 8):
        tid = (me + o) % 8
        pl.semaphore_signal(barrier, inc=1, device_id=(tid // 4, tid % 4), device_id_type=MESH)
    pl.semaphore_wait(barrier, 7)

    mats = ((wu, wou, 0), (wd, wod, 0), (wu, wou, 1), (wd, wod, 1))

    def chunk(ref, m, q, sub):
        k = mats[m][2]
        size = ref.shape[1] // 4
        part = size // SUBS
        return ref.at[k, pl.ds(aligned(q * size + sub * part, part), part), :]

    def w_y(m, sub):
        return remote(chunk(mats[m][0], m, dd, sub), chunk(mats[m][1], m, dd, sub),
                      w_snd.at[m, sub, 0], w_rcv.at[m, sub, 0], ynb)

    def w_x(m, sub):
        c = chunk(mats[m][1], m, dd, sub)
        return remote(c, c, w_snd.at[m, sub, 1], w_rcv.at[m, sub, 1], xnb)

    def w_c(m, sub):
        c = chunk(mats[m][1], m, dd, sub)
        return remote(c, c, w_snd.at[m, sub, 2], w_rcv.at[m, sub, 2], sib)

    def w_f(m, sub):
        c = chunk(mats[m][1], m, d_far, sub)
        return remote(c, c, w_snd.at[m, sub, 3], w_rcv.at[m, sub, 3], sib)

    def w_from(m, sub, which):
        q = (dd, d_far, d_sib, d_diag)[which]
        c = chunk(mats[m][1], m, q, sub)
        return remote(c, c, w_snd.at[m, sub, which], w_rcv.at[m, sub, which], sib)

    def got_y(m, sub):
        def fn():
            w_from(m, sub, 0).wait_recv()
            w_x(m, sub).start()
            w_c(m, sub).start()
        return fn

    def got_x(m, sub):
        def fn():
            w_from(m, sub, 1).wait_recv()
            w_f(m, sub).start()
        return fn

    def got_rest(m):
        def fn():
            for sub in range(SUBS):
                w_from(m, sub, 2).wait_recv()
                w_from(m, sub, 3).wait_recv()
        return fn

    def w_copies(kind, hf, k, pair):
        out = []
        for b in range(2):
            if kind == "u":
                src = (wu, wou)[hf].at[k, :, pl.ds(b * dim, dim)]
            else:
                src = (wd, wod)[hf].at[k, pl.ds(b * dim, dim), :]
            out.append(local(src, wb.at[2 * pair + b], s_w.at[2 * pair + b]))
        return out

    def w_load(kind, hf, k, pair):
        def fn():
            for c in w_copies(kind, hf, k, pair):
                c.start()
        return fn

    def w_wait(kind, hf, k, pair):
        def fn():
            for c in w_copies(kind, hf, k, pair):
                c.wait()
        return fn

    def run_loop(n, body, hooks):
        def f(it, carry):
            for key in sorted(hooks):
                @pl.when(it == key)
                def _(key=key):
                    for fn in hooks[key]:
                        fn()
            body(it)
            return carry
        lax.fori_loop(0, n, f, 0)

    def rslice(r):
        return pl.ds(aligned(r * bm, bm), bm)

    def x_copy(r):
        return local(x.at[pl.ds(aligned(row0 + r * bm, bm), bm), :], res.at[rslice(r), :], s_x.at[r])

    def act_out(dst, it, half0, b, buf):
        hf = half0 + it // nr
        return local(outs.at[buf], dst.at[hf, rslice(it % nr), pl.ds(b * dim, dim)], s_out.at[buf])

    def z_stage(nh, half0, pair0, z_dst, a_dst, hooks, wait_x=False):
        def epi(slot, zi, n):
            zb = gacc[slot, :bm, n].astype(BF16)
            outs[zi, :, n] = zb
            zf = zb.astype(F32)
            outs[zi + 1, :, n] = (zf * gelu_half(zf)).astype(BF16)

        def put(it, b):
            return (act_out(z_dst, it, half0, b, 2 * b), act_out(a_dst, it, half0, b, 2 * b + 1))

        def body(it):
            r = it % nr
            base = 2 * (pair0 + it // nr)
            if wait_x:
                x_copy(r).wait()

            @pl.when(it >= 2)
            def _():
                for c in put(it - 2, 1):
                    c.wait()
            for n in chunks:
                gacc[0, :bm, n] = dot_nn(res[rslice(r), :], wb[base, :, n])
                epi(1, 2, n)

            @pl.when(it >= 1)
            def _():
                for c in put(it - 1, 1):
                    c.start()
                for c in put(it - 1, 0):
                    c.wait()
            for n in chunks:
                gacc[1, :bm, n] = dot_nn(res[rslice(r), :], wb[base + 1, :, n])
                epi(0, 0, n)
            for c in put(it, 0):
                c.start()

        total = nr * nh
        run_loop(total, body, hooks)
        for c in put(total - 2, 1):
            c.wait()
        for n in chunks:
            epi(1, 2, n)
        for c in put(total - 1, 1):
            c.start()
        for c in put(total - 1, 0) + put(total - 1, 1):
            c.wait()

    def k_tiles(src, hf, r):
        return [local(src.at[hf, rslice(r), pl.ds(b * dim, dim)], ring.at[(r % 2) * 2 + b], s_ring.at[(r % 2) * 2 + b])
                for b in range(2)]

    def k_first(src, hf):
        def fn():
            for c in k_tiles(src, hf, 0):
                c.start()
        return fn

    def k_stage(src, hf, pair, trans, last, store, hooks):
        def part(r):
            if last:
                return local(hpart.at[rslice(r), :], gacc.at[r % 2, pl.ds(0, bm), :], s_gacc.at[r % 2])
            return local(gacc.at[r % 2, pl.ds(0, bm), :], hpart.at[rslice(r), :], s_gacc.at[r % 2])

        def keep(r):
            return local(res.at[rslice(r), :], hbuf.at[rslice(r), :], s_out.at[r % 2])

        if last:
            part(0).start()

        def body(r):
            slot = r % 2

            @pl.when(r + 1 < nr)
            def _():
                for c in k_tiles(src, hf, r + 1):
                    c.start()
                if last:
                    part(r + 1).start()
            for c in k_tiles(src, hf, r):
                c.wait()
            if last:
                part(r).wait()
                if store:
                    @pl.when(r >= 2)
                    def _():
                        keep(r - 2).wait()
            else:
                @pl.when(r >= 2)
                def _():
                    part(r - 2).wait()
            for n in chunks:
                if trans:
                    val = dot_nt(ring[slot * 2], wb[2 * pair, n, :]) + dot_nt(ring[slot * 2 + 1], wb[2 * pair + 1, n, :])
                else:
                    val = dot_nn(ring[slot * 2], wb[2 * pair, :, n]) + dot_nn(ring[slot * 2 + 1], wb[2 * pair + 1, :, n])
                if last:
                    res[rslice(r), n] = (val + gacc[slot, :bm, n]).astype(BF16)
                else:
                    gacc[slot, :bm, n] = val
            if not last:
                part(r).start()
            elif store:
                keep(r).start()

        run_loop(nr, body, hooks)
        if not last:
            part(nr - 2).wait()
            part(nr - 1).wait()
        elif store:
            keep(nr - 2).wait()
            keep(nr - 1).wait()

    def q_tile(src, it, b):
        buf = 2 * b + it % 2
        return local(src.at[it // nr, rslice(it % nr), pl.ds(b * dim, dim)], ring.at[buf], s_ring.at[buf])

    def q_first(src):
        def fn():
            q_tile(src, 0, 0).start()
        return fn

    def q_stage(z_src, q_dst, hooks):
        total = 2 * nr

        def epi(slot, buf, tile, n):
            e = gacc[slot, :bm, n].astype(BF16).astype(F32)
            outs[buf, :, n] = (e * gelu_slope(ring[tile, :, n].astype(F32))).astype(BF16)

        def body(it):
            r = it % nr
            base = 2 * (it // nr)
            q_tile(z_src, it, 1).start()

            @pl.when(it + 1 < total)
            def _():
                q_tile(z_src, it + 1, 0).start()

            @pl.when(it >= 1)
            def _():
                q_tile(z_src, it - 1, 1).wait()

            @pl.when(it >= 2)
            def _():
                act_out(q_dst, it - 2, 0, 1, 2).wait()
            for n in chunks:
                gacc[0, :bm, n] = dot_nt(res[rslice(r), :], wb[base, n, :])
                epi(1, 2, 2 + (it + 1) % 2, n)

            @pl.when(it >= 1)
            def _():
                act_out(q_dst, it - 1, 0, 1, 2).start()
                act_out(q_dst, it - 1, 0, 0, 0).wait()
            q_tile(z_src, it, 0).wait()
            for n in chunks:
                gacc[1, :bm, n] = dot_nt(res[rslice(r), :], wb[base + 1, n, :])
                epi(0, 0, it % 2, n)
            act_out(q_dst, it, 0, 0, 0).start()

        run_loop(total, body, hooks)
        act_out(q_dst, total - 2, 0, 1, 2).wait()
        q_tile(z_src, total - 1, 1).wait()
        for n in chunks:
            epi(1, 2, 2 + (total - 1) % 2, n)
        act_out(q_dst, total - 1, 0, 1, 2).start()
        act_out(q_dst, total - 1, 0, 0, 0).wait()
        act_out(q_dst, total - 1, 0, 1, 2).wait()

    alpha, beta = pl.ds(0, quart), pl.ds(quart, quart)

    def c_msg(k, t):
        return remote(pss.at[k, t], rc.at[k, t], g_snd.at[k, t], g_rcv.at[k, t], sib)

    def x_msg(k, i):
        src = (psm.at[k, 0, alpha], psm.at[k, 1, alpha], x3.at[k, 0])[i]
        return remote(src, rx.at[k, i], g_snd.at[k, 4 + i], g_rcv.at[k, 4 + i], xnb)

    def y_msg(k, i):
        src = (psm.at[k, 0, beta], psm.at[k, 2, beta], x3.at[k, 1])[i]
        return remote(src, ry.at[k, i], g_snd.at[k, 7 + i], g_rcv.at[k, 7 + i], ynb)

    def piece_of(s):
        ge3 = (s + 5) // 8
        eq4 = ((4 - s % 4) // 4) * ((s + 7) // 8)
        mine = ge3 - eq4
        t = mine * (s - 3 - s // 5) + (1 - mine) * (s - s // 4)
        oth = 1 - t % 2
        xr = 1 - t // 2
        return mine, oth, xx + xr * (1 - 2 * xx), (1 - cc) + mine * (2 * cc - 1)

    def g_tile(k, src, u):
        _, oth, xp, cp = piece_of(u // 2)
        krow = pl.ds(aligned((u % 2) * kr, kr), kr)
        if IS_UP[k]:
            return local(src.at[oth, krow, pl.ds(aligned(cp * dim, dim), dim)], gs.at[u % 2], s_gs.at[u % 2])
        col = pl.ds(aligned(xp * dim + cp * half, half), half)
        return local(src.at[oth, krow, col], gs.at[u % 2, :, pl.ds(0, half)], s_gs.at[u % 2])

    def g_first(k, src):
        def fn():
            g_tile(k, src, 0).start()
        return fn

    def res_copy(kind, h):
        rs = pl.ds(h * kr, kr)
        if kind == "h":
            src = hbuf.at[rs, :]
        else:
            src = (x if kind == "x" else dy).at[pl.ds(aligned(row0 + h * kr, kr), kr), :]
        return local(src, res.at[rs, :], s_res.at[h])

    def res_load(kind, h):
        def fn():
            res_copy(kind, h).start()
        return fn

    def g_stage(k, src, res_kind, hooks):
        def init(s):
            kind, t = PIECES[s]
            return local(zeros if kind == "s" else rc.at[k, t], gacc.at[s % 2], s_gacc.at[s % 2])

        def save(s):
            kind, t = PIECES[s]
            return local(gacc.at[s % 2], (pss if kind == "s" else psm).at[k, t], s_ps)

        init(0).start()
        init(1).start()
        hooks = {key: list(val) for key, val in hooks.items()}

        def before(s):
            def fn():
                init(s).wait()
                if s >= 1:
                    save(s - 1).start()
            return fn

        def after(s):
            def fn():
                save(s - 1).wait()
                kind, t = PIECES[s - 1]
                if kind == "s":
                    c_msg(k, t).start()
                elif t == 0:
                    x_msg(k, 0).start()
                    y_msg(k, 0).start()
                elif t == 1:
                    x_msg(k, 1).start()
                elif t == 2:
                    y_msg(k, 1).start()
                if s + 1 < 8:
                    kind, t = PIECES[s + 1]
                    if kind == "m":
                        c_msg(k, t).wait_recv()
                    init(s + 1).start()
            return fn

        for s in range(8):
            hooks.setdefault(2 * s, []).append(before(s))
            if s >= 1:
                hooks.setdefault(2 * s + 1, []).append(after(s))
        if res_kind is not None:
            for h in range(2):
                hooks.setdefault(h, []).append(lambda h=h: res_copy(res_kind, h).wait())

        def body(u):
            @pl.when(u + 1 < 16)
            def _():
                g_tile(k, src, u + 1).start()
            g_tile(k, src, u).wait()
            slot = (u // 2) % 2
            krow = pl.ds(aligned((u % 2) * kr, kr), kr)
            if IS_UP[k]:
                _, _, xp, _ = piece_of(u // 2)
                gacc[slot] += dot_tn(res[krow, pl.ds(aligned(xp * half, half), half)], gs[u % 2])
            else:
                gacc[slot] += dot_tn(gs[u % 2, :, :half], res[krow, :])

        run_loop(16, body, hooks)
        save(7).start()
        save(7).wait()

    nq = quart // 8

    def side_add(dst, a, b):
        side[dst] = side[a] + side[b]

    def side_scale(dst, parts):
        def f(i, acc):
            rs = pl.ds(aligned(i * 8, 8), 8)
            v = side[parts[0], rs, :]
            for p in parts[1:]:
                v = v + side[p, rs, :]
            v = v * 0.25
            side[dst, rs, :] = v
            v = v * v
            for n in range(0, dim, 128):
                acc = acc + v[:, n:n + 128]
            return acc
        ss[...] = lax.fori_loop(0, nq, f, ss[...])

    def side_in(i, src):
        return local(src, side.at[i], s_side.at[i])

    def side_out(i, dst):
        return local(side.at[i], dst, s_side.at[i])

    def join_phases(k):
        ins = ((0, psm.at[k, 1, beta]), (1, ry.at[k, 0]), (2, psm.at[k, 2, alpha]), (3, rx.at[k, 0]))

        def pa():
            x_msg(k, 0).wait_recv()
            y_msg(k, 0).wait_recv()
            for i, s in ins:
                side_in(i, s).start()

        def pb():
            for i, s in ins:
                side_in(i, s).wait()
            side_add(0, 0, 1)
            side_add(2, 2, 3)
            side_out(0, x3.at[k, 0]).start()
            side_out(2, x3.at[k, 1]).start()

        def pc():
            side_out(0, x3.at[k, 0]).wait()
            side_out(2, x3.at[k, 1]).wait()
            x_msg(k, 2).start()
            y_msg(k, 2).start()
        return pa, pb, pc

    def to_sib(k):
        g = gfin.at[k, pl.ds(aligned((1 - cc) * quart, quart), quart), :]
        return remote(g, gsib.at[k // 2], f_snd.at[k // 2], f_rcv.at[k // 2], sib)

    def final_phases(k):
        ina = ((0, psm.at[k, 3, alpha]), (1, rx.at[k, 1]), (2, ry.at[k, 2]))
        inb = ((0, psm.at[k, 3, beta]), (1, ry.at[k, 1]), (2, rx.at[k, 2]))

        def pa():
            x_msg(k, 1).wait_recv()
            y_msg(k, 2).wait_recv()
            for i, s in ina:
                side_in(i, s).start()

        def pb():
            for i, s in ina:
                side_in(i, s).wait()
            side_scale(3, (0, 1, 2))
            side_out(3, gfin.at[k, alpha]).start()
            y_msg(k, 1).wait_recv()
            x_msg(k, 2).wait_recv()
            for i, s in inb:
                side_in(i, s).start()

        def pc():
            side_out(3, gfin.at[k, alpha]).wait()
            for i, s in inb:
                side_in(i, s).wait()
            side_scale(0, (0, 1, 2))
            side_out(0, gfin.at[k, beta]).start()

        def pd():
            side_out(0, gfin.at[k, beta]).wait()
            if IS_UP[k]:
                to_sib(k).start()
        return pa, pb, pc, pd

    def at(first, fns):
        return {first + i: [fn] for i, fn in enumerate(fns)}

    def merge(*tables):
        out = {}
        for table in tables:
            for key, fns in table.items():
                out.setdefault(key, []).extend(fns)
        return out

    ss[...] = jnp.zeros_like(ss)
    for m in range(2):
        for sub in range(SUBS):
            w_y(m, sub).start()
    w_load("u", 0, 0, 0)()
    for r in range(nr):
        x_copy(r).start()
    w_load("d", 0, 0, 1)()
    for m in range(2, 4):
        for sub in range(SUBS):
            w_y(m, sub).start()

    w_wait("u", 0, 0, 0)()
    z_stage(1, 0, 0, z1, a1, merge({5 * nr // 8: [got_y(0, 0)]}, {nr - 1: [k_first(a1, 0)]}), wait_x=True)
    w_wait("d", 0, 0, 1)()
    k_stage(a1, 0, 1, False, False, False, merge(
        {2 * nr // 8: [got_y(0, 1)]}, {3 * nr // 8: [got_x(0, 0)]}, {7 * nr // 8: [got_y(1, 0), got_x(0, 1)]}))
    got_rest(0)()
    w_load("u", 1, 0, 0)()
    w_wait("u", 1, 0, 0)()
    z_stage(1, 1, 0, z1, a1, merge(
        {4 * nr // 8: [got_y(1, 1), got_x(1, 0)]}, {7 * nr // 8: [got_y(2, 0)]}, {nr - 1: [k_first(a1, 1)]}))
    got_x(1, 1)()
    got_rest(1)()
    w_load("d", 1, 0, 1)()
    w_load("u", 0, 1, 0)()
    w_wait("d", 1, 0, 1)()
    k_stage(a1, 1, 1, False, True, True, merge(
        {4 * nr // 8: [got_y(2, 1), got_x(2, 0)]}, {7 * nr // 8: [got_y(3, 0)]}))
    w_wait("u", 0, 1, 0)()

    def w3_other():
        got_x(2, 1)()
        got_rest(2)()
        w_load("u", 1, 1, 1)()
    z_stage(2, 0, 0, z3, a3, merge(
        {nr - 2: [w3_other]}, {nr: [w_wait("u", 1, 1, 1)]}, {nr + 1: [got_y(3, 1), got_x(3, 0)]},
        {2 * nr - nr // 2: [res_load("dy", 0)]}, {2 * nr - 1: [g_first(0, a3)]}))
    res_load("dy", 1)()
    w_load("d", 0, 1, 0)()

    def w4_other():
        got_x(3, 1)()
        got_rest(3)()
        w_load("d", 1, 1, 1)()
    g_stage(0, a3, "dy", merge({4: [w4_other]}, {14: [q_first(z3)]}))
    w_wait("d", 0, 1, 0)()
    q_stage(z3, q3, merge(
        {nr: [w_wait("d", 1, 1, 1)]}, at(4, join_phases(0)),
        {2 * nr - nr // 2: [res_load("h", 0)]}, {2 * nr - 1: [g_first(1, q3)]}))
    res_load("h", 1)()
    w_load("u", 0, 1, 0)()
    w_load("u", 1, 1, 1)()
    g_stage(1, q3, "h", {14: [k_first(q3, 0)]})
    w_wait("u", 0, 1, 0)()
    k_stage(q3, 0, 0, True, False, False, merge(at(4, final_phases(0)), {nr - 1: []}))
    k_first(q3, 1)()
    w_wait("u", 1, 1, 1)()
    k_stage(q3, 1, 1, True, True, False, at(1, join_phases(1)))
    w_load("d", 0, 0, 0)()
    w_load("d", 1, 0, 1)()
    g_first(2, a1)()
    g_stage(2, a1, None, {14: [q_first(z1)]})
    w_wait("d", 0, 0, 0)()
    q_stage(z1, q1, merge(
        {nr: [w_wait("d", 1, 0, 1)]}, at(0, final_phases(1)), at(5, join_phases(2)),
        {2 * nr - nr // 2: [res_load("x", 0)]}, {2 * nr - 1: [g_first(3, q1)]}))
    res_load("x", 1)()
    g_stage(3, q1, "x", at(10, final_phases(2)))
    for fn in join_phases(3):
        fn()
    for fn in final_phases(3):
        fn()

    nbuf[me] = ss[...]

    def n_send(o):
        tid = (me + o) % 8
        return remote(ss, nbuf.at[me], n_snd.at[o], n_rcv.at[o], (tid // 4, tid % 4))

    def n_recv(o):
        return remote(ss, nbuf.at[(me + 8 - o) % 8], n_snd.at[o], n_rcv.at[o], sib)

    for o in range(1, 8):
        n_send(o).start()
    for o in range(1, 8):
        n_recv(o).wait_recv()
    acc = nbuf[0]
    for i in range(1, 8):
        acc = acc + nbuf[i]
    nrm[...] = acc

    for k in (1, 3):
        to_sib(k).wait_recv()
        to_sib(k).wait_send()
    for o in range(1, 8):
        n_send(o).wait_send()
    for m in range(4):
        for sub in range(SUBS):
            for c in (w_y(m, sub), w_x(m, sub), w_c(m, sub), w_f(m, sub)):
                c.wait_send()
    for k in range(4):
        for t in range(4):
            c_msg(k, t).wait_send()
        for i in range(3):
            x_msg(k, i).wait_send()
            y_msg(k, i).wait_send()


def gradients(act_in, grad_out, w_up, w_down):
    rows = act_in.shape[0] // 2
    dim = act_in.shape[1]
    wide = w_up.shape[2]
    half, quart = dim // 2, dim // 4
    bm = rows // 8
    hbm = pltpu.HBM
    S = jax.ShapeDtypeStruct
    act = S((2, rows, wide), BF16)
    outs = [
        S((4, half, dim), F32), S((2, quart, dim), F32), S((8, 128), F32),
        S(w_up.shape, BF16), S(w_down.shape, BF16), act, act, act, act, act, act,
        S((rows, dim), BF16), S((rows, dim), F32),
        S((4, 4, half, dim), F32), S((4, 4, half, dim), F32), S((4, 4, half, dim), F32),
        S((4, 3, quart, dim), F32), S((4, 3, quart, dim), F32), S((4, 2, quart, dim), F32),
    ]
    out_specs = [pl.BlockSpec(memory_space=hbm) for _ in outs]
    out_specs[2] = pl.BlockSpec(memory_space=pltpu.VMEM)
    dma = pltpu.SemaphoreType.DMA
    scratch = [
        pltpu.VMEM((4, dim, dim), BF16), pltpu.VMEM((4, bm, dim), BF16), pltpu.VMEM((2, half, dim), F32),
        pltpu.VMEM((4, bm, dim), BF16), pltpu.VMEM((rows, dim), BF16), pltpu.VMEM((2, rows // 2, dim), BF16),
        pltpu.VMEM((4, quart, dim), F32), pltpu.VMEM((8, 128), F32), pltpu.VMEM((8, 8, 128), F32),
        dma((8,)), dma((4,)), dma((4,)), dma((4,)), dma((2,)), dma, dma((2,)), dma((2,)), dma((4,)),
        dma((4, SUBS, 4)), dma((4, SUBS, 4)), dma((4, 10)), dma((4, 10)), dma((2,)), dma((2,)), dma((8,)), dma((8,)),
    ]
    flops = 20 * rows * dim * 2 * wide
    return pl.pallas_call(
        functools.partial(grad_kernel, rows, bm, min(256, dim)),
        out_shape=outs,
        in_specs=[pl.BlockSpec(memory_space=hbm)] * 5,
        out_specs=out_specs,
        scratch_shapes=scratch,
        compiler_params=pltpu.CompilerParams(
            collective_id=0, has_side_effects=True, vmem_limit_bytes=66_900_000
        ),
        cost_estimate=pl.CostEstimate(flops=flops, bytes_accessed=1_500_000_000, transcendentals=0),
        name="grads",
    )(act_in, grad_out, w_up, w_down, jnp.zeros((half, dim), F32))[:3]


def solution(mesh):
    spec_rows = P("data", None)
    spec_wup = P(None, None, "model")
    spec_wdown = P(None, "model", None)
    spec_sup = P(None, "data", "model")
    spec_sdown = P(None, ("model", "data"), None)
    spec_scalar = P(None)

    def local_step(act_in, grad_out, w_up, w_down, master_up, master_down, mom_up, mom_down, var_up, var_down, learn_rate, clip_norm):
        gfin, gsib, squares = gradients(act_in, grad_out, w_up, w_down)
        core = lax.axis_index("data") % 2
        quart = gsib.shape[1]

        def up_grad(k):
            own = lax.dynamic_slice_in_dim(gfin[k], core * quart, quart, 0)
            other = gsib[k // 2]
            return jnp.concatenate([jnp.where(core == 0, own, other), jnp.where(core == 0, other, own)], axis=1)

        grad_up = jnp.stack([up_grad(3), up_grad(1)])
        grad_down = jnp.stack([gfin[2], gfin[0]])
        norm_val = jnp.sqrt(jnp.sum(squares))
        clip_scale = jnp.minimum(1.0, clip_norm[0] / (norm_val + NORM_EPS))
        lr_val = learn_rate[0]
        new_master_down, new_mom_down, new_var_down = adam_update(master_down, mom_down, var_down, grad_down, clip_scale, lr_val)
        new_w_down = lax.all_gather(new_master_down.astype(BF16), "data", axis=1, tiled=True)
        new_master_up, new_mom_up, new_var_up = adam_update(master_up, mom_up, var_up, grad_up, clip_scale, lr_val)
        new_w_up = lax.all_gather(new_master_up.astype(BF16), "data", axis=1, tiled=True)
        return (new_w_up, new_w_down, new_master_up, new_master_down, new_mom_up, new_mom_down, new_var_up, new_var_down, norm_val.reshape(1))

    return jax.shard_map(local_step, mesh=mesh, in_specs=(spec_rows, spec_rows, spec_wup, spec_wdown, spec_sup, spec_sdown, spec_sup, spec_sdown, spec_sup, spec_sdown, spec_scalar, spec_scalar), out_specs=(spec_wup, spec_wdown, spec_sup, spec_sdown, spec_sup, spec_sdown, spec_sup, spec_sdown, spec_scalar), check_vma=False)
```

time: 3030 us -> 1300 us (0.43)
  blocking collectives: 1910 us -> 0 us
  Pallas kernels: 0 us -> 1060 us
  matrix products: 765 us -> 0 us
  local copies, waits for them, and re-layouts: 109 us -> 28.5 us
    psum x3 -> x0, blocking collectives: 1910 us -> none  [the longest x1 950 us: local_grads(): hid_two = lax.psum(hid_part, 'model').astype(jnp.bfloat16)]
    pallas_call x0 -> x1, Pallas kernels: none -> 1060 us  [gradients(): pl.pallas_call(functools.partial(grad_kernel, rows, bm, min(256, dim)), o...]
    dot_general x9 -> x0, matrix products: 701 us -> none  [the longest x1 110 us: local_grads(): jnp.einsum('bd,fd->bf', dhid_two, w_down[0], preferred_element_type=jnp.f...]
    unnamed x13 -> x12, local copies, waits for them, and re-layouts: 98.2 us -> 17.7 us
    unnamed x1 -> x0, matrix products: 63.5 us -> none
    unnamed x8 -> x2, waiting for transfers between devices: 56 us -> 0.03 us
    all_gather x2, waiting for transfers between devices: 117 us -> 153 us  [the longest x1 84.5 us: local_step(): lax.all_gather(new_master_down.astype(BF16), 'data', axis=1, tiled=True)]
  transfers between devices with their start and end apart: 6 -> 2, of which waited for: 3 -> 2; matrix products, arithmetic and copies ran while one was open for 16% -> 1% of each run, Pallas kernels for 0% -> 0%
where the time goes in v1:
time: 1300 us; the launch traced here: 1290 us
  Pallas kernels  1060 us (82%)
  waiting for transfers between devices  153 us (12%)
  other arithmetic  35 us (3%)
  local copies, waits for them, and re-layouts  28.5 us (2%)
  between operations  17.7 us (1%)
    pallas_call x1, Pallas kernels, gradients(): pl.pallas_call(functools.partial(grad_kernel, rows, bm, min(256, dim)), o...  1060 us
    all_gather x1, waiting for transfers between devices, local_step(): lax.all_gather(new_master_down.astype(BF16), 'data', axis=1, tiled=True)  84.5 us
    all_gather x1, waiting for transfers between devices, local_step(): lax.all_gather(new_master_up.astype(BF16), 'data', axis=1, tiled=True)  68.8 us
  transfers between devices with their start and end apart: 2, of which 2 were waited for; matrix products, arithmetic and copies ran while one was open for 1% of the time, Pallas kernels for 0%

profile of v1, /device:TPU:0, one launch (start us, length us, event | category | flops | bytes accessed | tf_op | source)
XLA Modules:
  0.0 1293.4 jit_solution(18269753261206096932)
XLA Ops:
  7.2 0.0 all-gather.3.cloned.1.call-start
  7.9 1.9 broadcast_in_dim.3.zeros
  9.8 1058.7 %grads.1 = (f32[4,640,1280]{2,1,0:T(8,128)}, f32[2,320,1280]{2,1,0:T(8,128)}, f32[8,128]{1,0:T(8,128)}, bf16[2,1280,2560]{2,1,0:T(8,128)(2,1)}, bf16[2,2560,1280...) custom-call(bf16[8192,1280]{1,0:T(8,128)(2,1)} %x.1, ...), custom_call_target="tpu_custom_call" | custom-call | flops 536870912000 | bytes 1500000000 | tf_op jit(solution)/shard_map/grads/pallas_call | solution.py:703
  1068.5 0.0 copy-start
  1068.5 8.9 fusion.6
  1078.0 0.0 copy-done
  1078.0 0.6 reduce_sum.9
  1079.4 3.4 select_bitcast_fusion.3
  1082.8 2.1 maximum_bitcast_fusion
  1084.9 14.4 %fusion.4 = (bf16[2,320,2560]{2,1,0:T(8,128)(2,1)}, f32[2,320,2560]{2,1,0:T(8,128)}, f32[2,320,2560]{2,1,0:T(8,128)}, f32[2,320,2560]{2,1,0:T(8,128)}) fusion(f32[2,320,2560]{2,1,0:T(8,128)} %param.16, f32[]{:T(128)} %bitcast.7, f32[1,320,2560]{2,1,0:T(8,128)} %get-tuple-element.34, f32[1,320,2560]{2,1,0:T(8,128)S(1)} %get-tuple-element.33, ...), kind=kLoop, calls=%fused_computation.17 | loop fusion | flops 24576000 | bytes 49152008 | tf_op jit(solution)/shard_map/convert_element_type | solution.py:743
  1099.3 0.0 all-gather.3.cloned.1.call-update
  1099.4 0.0 all-gather.5.cloned.1.call-start
  1099.4 14.4 %fusion.2 = (bf16[2,640,1280]{2,1,0:T(8,128)(2,1)}, f32[2,640,1280]{2,1,0:T(8,128)}, f32[2,640,1280]{2,1,0:T(8,128)}, f32[2,640,1280]{2,1,0:T(8,128)}) fusion(f32[2,640,1280]{2,1,0:T(8,128)} %param.17, f32[]{:T(128)} %bitcast.7, f32[1,640,1280]{2,1,0:T(8,128)} %get-tuple-element.24, f32[1,640,1280]{2,1,0:T(8,128)S(1)} %get-tuple-element.23, ...), kind=kLoop, calls=%fused_computation.16 | loop fusion | flops 24576000 | bytes 49152008 | tf_op jit(solution)/shard_map/convert_element_type | solution.py:741
  1113.8 0.0 all-gather.5.cloned.1.call-update
  1113.8 68.8 %all-gather.3.cloned.1.call-done = bf16[2,1280,2560]{2,1,0:T(8,128)(2,1)} async-done(((bf16[2,320,2560]{2,1,0:T(8,128)(2,1)}), bf16[2,1280,2560]{2,1,0:T(8,128)(2,1)}) %all-gather.3.cloned.1.call-update) | async-done | bytes 13107216 | tf_op jit(solution)/shard_map/all_gather | solution.py:743
  1182.7 84.5 %all-gather.5.cloned.1.call-done = bf16[2,2560,1280]{2,1,0:T(8,128)(2,1)} async-done(((bf16[2,640,1280]{2,1,0:T(8,128)(2,1)}), bf16[2,2560,1280]{2,1,0:T(8,128)(2,1)}) %all-gather.5.cloned.1.call-update) | async-done | bytes 13107216 | tf_op jit(solution)/shard_map/all_gather | solution.py:741
  1267.2 0.0 slice-start
  1267.2 0.0 slice-start.1
  1267.2 0.0 slice-start.2
  1267.2 0.0 slice-start.3
  1267.2 12.5 copy.25
  1279.8 0.0 slice-done
  1279.8 0.0 slice-done.1
  1279.8 0.0 slice-done.2
  1279.8 0.2 slice-done.3
  1280.0 4.9 copy.26
  (1 shorter events, 0.0 us)
Async XLA Ops:
  7.2 1175.5 %all-gather.3.cloned.1.call-start = ((), (), s32[]{:S(2)}) async-start(), calls=%async_computation | async-start | bytes 16384000 | tf_op jit(solution)/shard_map/all_gather | solution.py:743
  1068.5 9.5 copy-start
  1099.4 167.8 %all-gather.5.cloned.1.call-start = ((), (), s32[]{:S(2)}) async-start(), calls=%async_computation.1 | async-start | bytes 16384000 | tf_op jit(solution)/shard_map/all_gather | solution.py:741
  1267.2 12.5 slice-start
  1267.2 12.5 slice-start.1
  1267.2 12.5 slice-start.2
  1267.2 12.8 slice-start.3
Sparse Core Ops, SparseCore 0:
  1099.5 83.1 all-gather.2
  1184.2 82.9 all-gather.4

commit v2 on v1

v2 whole, which is shorter than its diff:
```python
import functools

import jax
import jax.numpy as jnp
from jax import lax
from jax.experimental import pallas as pl
from jax.experimental.pallas import tpu as pltpu
from jax.sharding import PartitionSpec as P


STEP = 10
BETA_ONE = 0.9
BETA_TWO = 0.95
ADAM_EPS = 1e-8
NORM_EPS = 1e-6
MESH = pl.DeviceIdType.MESH
F32 = jnp.float32
BF16 = jnp.bfloat16
GELU_ONE = 0.7978845608028654
GELU_TWO = GELU_ONE * 0.044715
IS_UP = (False, True, False, True)
LONG = (("s", 0), ("s", 1), ("m", 0), ("s", 2), ("m", 1), ("s", 3), ("m", 2), ("m", 3))
SHORT = (("s", 0), ("s", 1), ("m", 0), ("s", 2), ("m", 1), ("m", 2))
SUBS = 2


def gelu_half(z):
    return 0.5 + 0.5 * jnp.tanh(z * (GELU_ONE + GELU_TWO * (z * z)))


def gelu_slope(z):
    square = z * z
    t = jnp.tanh(z * (GELU_ONE + GELU_TWO * square))
    ramp = z * (0.5 * GELU_ONE + (1.5 * GELU_TWO) * square)
    return (1.0 + t) * (0.5 + (1.0 - t) * ramp)


def dot_nn(a, b):
    return jnp.dot(a, b, preferred_element_type=F32)


def dot_nt(a, b):
    return lax.dot_general(a, b, (((1,), (1,)), ((), ())), preferred_element_type=F32)


def dot_tn(a, b):
    return lax.dot_general(a, b, (((0,), (0,)), ((), ())), preferred_element_type=F32)


def grad_kernel(
    rows, bm, bz, nc,
    x, dy, wu, wd,
    gfin, gsib, nrm, wou, wod, z1, a1, z3, a3, q3, q1, hbuf, ebuf, hpart, psm, rc, rx, ry, x3,
    wb, ring, gacc, outs, res, gs, side, ss, nbuf,
    s_x, s_w, s_ring, s_out, s_gacc, s_ps, s_res, s_gs, s_side,
    w_snd, w_rcv, g_snd, g_rcv, f_snd, f_rcv, n_snd, n_rcv,
):
    yy = lax.axis_index("model")
    dd = lax.axis_index("data")
    xx = dd // 2
    cc = dd % 2
    me = yy * 4 + dd
    d_sib = 2 * xx + (1 - cc)
    d_far = 2 * (1 - xx) + cc
    d_diag = 2 * (1 - xx) + (1 - cc)
    sib, xnb, ynb = (yy, d_sib), (yy, d_far), (1 - yy, dd)
    dim = x.shape[1]
    half = dim // 2
    quart = dim // 4
    nr = rows // bm
    nz = rows // bz
    kr = rows // 2
    row0 = yy * rows
    chunks = [slice(n, n + nc) for n in range(0, dim, nc)]

    def aligned(v, m):
        return pl.multiple_of(v, m)

    def local(src, dst, sem):
        return pltpu.make_async_copy(src, dst, sem)

    def remote(src, dst, snd, rcv, dev):
        return pltpu.make_async_remote_copy(
            src_ref=src, dst_ref=dst, send_sem=snd, recv_sem=rcv, device_id=dev, device_id_type=MESH
        )

    def meet():
        barrier = pltpu.get_barrier_semaphore()
        for o in range(1, 8):
            tid = (me + o) % 8
            pl.semaphore_signal(barrier, inc=1, device_id=(tid // 4, tid % 4), device_id_type=MESH)
        pl.semaphore_wait(barrier, 7)

    mats = ((wu, wou, 0), (wd, wod, 0), (wu, wou, 1), (wd, wod, 1))

    def chunk(ref, m, q, sub):
        k = mats[m][2]
        size = ref.shape[1] // 4
        part = size // SUBS
        return ref.at[k, pl.ds(aligned(q * size + sub * part, part), part), :]

    def w_y(m, sub):
        return remote(chunk(mats[m][0], m, dd, sub), chunk(mats[m][1], m, dd, sub),
                      w_snd.at[m, sub, 0], w_rcv.at[m, sub, 0], ynb)

    def w_x(m, sub):
        c = chunk(mats[m][1], m, dd, sub)
        return remote(c, c, w_snd.at[m, sub, 1], w_rcv.at[m, sub, 1], xnb)

    def w_c(m, sub):
        c = chunk(mats[m][1], m, dd, sub)
        return remote(c, c, w_snd.at[m, sub, 2], w_rcv.at[m, sub, 2], sib)

    def w_f(m, sub):
        c = chunk(mats[m][1], m, d_far, sub)
        return remote(c, c, w_snd.at[m, sub, 3], w_rcv.at[m, sub, 3], sib)

    def w_from(m, sub, which):
        q = (dd, d_far, d_sib, d_diag)[which]
        c = chunk(mats[m][1], m, q, sub)
        return remote(c, c, w_snd.at[m, sub, which], w_rcv.at[m, sub, which], sib)

    def got_y(m, sub):
        def fn():
            w_from(m, sub, 0).wait_recv()
            w_x(m, sub).start()
            w_c(m, sub).start()

        return fn

    def got_x(m, sub):
        def fn():
            w_from(m, sub, 1).wait_recv()
            w_f(m, sub).start()

        return fn

    def got_rest(m):
        def fn():
            for sub in range(SUBS):
                w_from(m, sub, 2).wait_recv()
                w_from(m, sub, 3).wait_recv()

        return fn

    def w_copies(kind, hf, k, pair):
        out = []
        for b in range(2):
            if kind == "u":
                src = (wu, wou)[hf].at[k, :, pl.ds(b * dim, dim)]
            else:
                src = (wd, wod)[hf].at[k, pl.ds(b * dim, dim), :]
            out.append(local(src, wb.at[2 * pair + b], s_w.at[2 * pair + b]))
        return out

    def w_load(kind, hf, k, pair):
        def fn():
            for c in w_copies(kind, hf, k, pair):
                c.start()

        return fn

    def w_wait(kind, hf, k, pair):
        def fn():
            for c in w_copies(kind, hf, k, pair):
                c.wait()

        return fn

    def run_loop(n, body, hooks):
        def f(it, carry):
            for key in sorted(hooks):
                @pl.when(it == key)
                def _(key=key):
                    for fn in hooks[key]:
                        fn()
            body(it)
            return carry

        lax.fori_loop(0, n, f, 0)

    def rslice(r):
        return pl.ds(aligned(r * bm, bm), bm)

    def zslice(r):
        return pl.ds(aligned(r * bz, bz), bz)

    def x_copy(r):
        return local(x.at[pl.ds(aligned(row0 + r * bz, bz), bz), :], res.at[zslice(r), :], s_x.at[r])

    def act_out(dst, it, half0, b, buf):
        hf = half0 + it // nz
        return local(outs.at[buf], dst.at[hf, zslice(it % nz), pl.ds(b * dim, dim)], s_out.at[buf])

    def out_waits(it, put):
        for c in put(it, 0, it):
            c.wait()

        @pl.when(it >= 1)
        def _():
            for c in put(it - 1, 1, it):
                c.wait()

    def out_starts(it, put):
        for c in put(it, 0, it):
            c.start()

        @pl.when(it >= 1)
        def _():
            for c in put(it - 1, 1, it):
                c.start()

    def z_stage(nh, half0, pair0, z_dst, a_dst, hooks, wait_x=False, ending=()):
        def epi(slot, zi, n):
            zb = gacc[slot, :bz, n].astype(BF16)
            outs[zi, :, n] = zb
            zf = zb.astype(F32)
            outs[zi + 1, :, n] = (zf * gelu_half(zf)).astype(BF16)

        def put(it, b, when):
            buf = 4 * (when % 2) + 2 * b
            return (act_out(z_dst, it, half0, b, buf), act_out(a_dst, it, half0, b, buf + 1))

        def body(it):
            r = it % nz
            base = 2 * (pair0 + it // nz)
            buf = 4 * (it % 2)
            if wait_x:
                x_copy(r).wait()

            @pl.when(it >= 2)
            def _():
                out_waits(it - 2, put)

            for n in chunks:
                gacc[0, :bz, n] = dot_nn(res[zslice(r), :], wb[base, :, n])
                epi(1, buf + 2, n)
            for n in chunks:
                gacc[1, :bz, n] = dot_nn(res[zslice(r), :], wb[base + 1, :, n])
                epi(0, buf, n)
            out_starts(it, put)

        total = nz * nh
        run_loop(total, body, hooks)
        for fn in ending:
            fn()
        out_waits(total - 2, put)
        for n in chunks:
            epi(1, 4 * (total % 2) + 2, n)
        for c in put(total - 1, 1, total):
            c.start()
        out_waits(total - 1, put)
        for c in put(total - 1, 1, total):
            c.wait()

    def k_tiles(src, hf, r):
        return [local(src.at[hf, rslice(r), pl.ds(b * dim, dim)], ring.at[(r % 2) * 2 + b], s_ring.at[(r % 2) * 2 + b])
                for b in range(2)]

    def k_first(src, hf):
        def fn():
            for c in k_tiles(src, hf, 0):
                c.start()

        return fn

    def k_stage(src, hf, pair, trans, store, hooks):
        last = store is not None

        def part(r):
            if last:
                return local(hpart.at[rslice(r), :], gacc.at[r % 2, pl.ds(0, bm), :], s_gacc.at[r % 2])
            return local(gacc.at[r % 2, pl.ds(0, bm), :], hpart.at[rslice(r), :], s_gacc.at[r % 2])

        def keep(r):
            return local(res.at[rslice(r), :], store.at[rslice(r), :], s_out.at[r % 2])

        if last:
            part(0).start()

        def body(r):
            slot = r % 2

            @pl.when(r + 1 < nr)
            def _():
                for c in k_tiles(src, hf, r + 1):
                    c.start()
                if last:
                    part(r + 1).start()

            for c in k_tiles(src, hf, r):
                c.wait()
            if last:
                part(r).wait()

                @pl.when(r >= 2)
                def _():
                    keep(r - 2).wait()
            else:
                @pl.when(r >= 2)
                def _():
                    part(r - 2).wait()
            for n in chunks:
                if trans:
                    val = dot_nt(ring[slot * 2], wb[2 * pair, n, :]) + dot_nt(ring[slot * 2 + 1], wb[2 * pair + 1, n, :])
                else:
                    val = dot_nn(ring[slot * 2], wb[2 * pair, :, n]) + dot_nn(ring[slot * 2 + 1], wb[2 * pair + 1, :, n])
                if last:
                    res[rslice(r), n] = (val + gacc[slot, :bm, n]).astype(BF16)
                else:
                    gacc[slot, :bm, n] = val
            if not last:
                part(r).start()
            else:
                keep(r).start()

        run_loop(nr, body, hooks)
        if not last:
            part(nr - 2).wait()
            part(nr - 1).wait()
        else:
            keep(nr - 2).wait()
            keep(nr - 1).wait()

    def q_tile(src, it, b):
        buf = 2 * b + it % 2
        return local(src.at[it // nz, zslice(it % nz), pl.ds(b * dim, dim)], ring.at[buf, pl.ds(0, bz), :], s_ring.at[buf])

    def q_first(src):
        def fn():
            q_tile(src, 0, 0).start()

        return fn

    def q_stage(z_src, q_dst, hooks, ending=()):
        total = 2 * nz

        def epi(slot, buf, tile, n):
            e = gacc[slot, :bz, n].astype(BF16).astype(F32)
            outs[buf, :, n] = (e * gelu_slope(ring[tile, :bz, n].astype(F32))).astype(BF16)

        def put(it, b, when):
            return (act_out(q_dst, it, 0, b, 4 * (when % 2) + 2 * b),)

        def body(it):
            r = it % nz
            base = 2 * (it // nz)
            buf = 4 * (it % 2)
            q_tile(z_src, it, 1).start()

            @pl.when(it + 1 < total)
            def _():
                q_tile(z_src, it + 1, 0).start()

            @pl.when(it >= 1)
            def _():
                q_tile(z_src, it - 1, 1).wait()

            @pl.when(it >= 2)
            def _():
                out_waits(it - 2, put)

            q_tile(z_src, it, 0).wait()
            for n in chunks:
                gacc[0, :bz, n] = dot_nt(res[zslice(r), :], wb[base, n, :])
                epi(1, buf + 2, 2 + (it + 1) % 2, n)
            for n in chunks:
                gacc[1, :bz, n] = dot_nt(res[zslice(r), :], wb[base + 1, n, :])
                epi(0, buf, it % 2, n)
            out_starts(it, put)

        run_loop(total, body, hooks)
        for fn in ending:
            fn()
        out_waits(total - 2, put)
        q_tile(z_src, total - 1, 1).wait()
        for n in chunks:
            epi(1, 4 * (total % 2) + 2, 2 + (total - 1) % 2, n)
        for c in put(total - 1, 1, total):
            c.start()
        out_waits(total - 1, put)
        for c in put(total - 1, 1, total):
            c.wait()

    alpha, beta = pl.ds(0, quart), pl.ds(quart, quart)

    def c_msg(k, t):
        slot = (LONG if k == 3 else SHORT).index(("s", t)) % 2 if k == 3 or t < 3 else 0
        return remote(gacc.at[slot], rc.at[k, t], g_snd.at[k, t], g_rcv.at[k, t], sib)

    def x_msg(k, i):
        src = (psm.at[k, 0, alpha], psm.at[k, 1, alpha], x3.at[k, 0])[i]
        return remote(src, rx.at[k, i], g_snd.at[k, 4 + i], g_rcv.at[k, 4 + i], xnb)

    def y_msg(k, i):
        src = (psm.at[k, 0, beta], psm.at[k, 2, beta], x3.at[k, 1])[i]
        return remote(src, ry.at[k, i], g_snd.at[k, 7 + i], g_rcv.at[k, 7 + i], ynb)

    def piece_of(s, count):
        v = s + s // (count - 1)
        mine = (1 - v % 2) * ((v + 7) // 8)
        t = mine * (v // 2 - 1) + (1 - mine) * ((v + 1) // 2)
        oth = 1 - t % 2
        xr = 1 - t // 2
        return mine, oth, xx + xr * (1 - 2 * xx), (1 - cc) + mine * (2 * cc - 1)

    def tile_of(k, src, u, oth, xp, cp):
        krow = pl.ds(aligned((u % 2) * kr, kr), kr)
        if IS_UP[k]:
            return local(src.at[oth, krow, pl.ds(aligned(cp * dim, dim), dim)], gs.at[u % 2], s_gs.at[u % 2])
        col = pl.ds(aligned(xp * dim + cp * half, half), half)
        return local(src.at[oth, krow, col], gs.at[u % 2, :, pl.ds(0, half)], s_gs.at[u % 2])

    def g_tile(k, src, u):
        _, oth, xp, cp = piece_of(u // 2, 8 if k == 3 else 6)
        return tile_of(k, src, u, oth, xp, cp)

    def g_first(k, src):
        def fn():
            g_tile(k, src, 0).start()

        return fn

    def g_dot(k, u, xp, n):
        krow = pl.ds(aligned((u % 2) * kr, kr), kr)
        if IS_UP[k]:
            return dot_tn(res[krow, pl.ds(aligned(xp * half, half), half)], gs[u % 2, :, n])
        return dot_tn(gs[u % 2, :, :half], res[krow, n])

    def res_copy(kind, h):
        rs = pl.ds(h * kr, kr)
        if kind in ("h", "e"):
            src = (hbuf if kind == "h" else ebuf).at[rs, :]
        else:
            src = (x if kind == "x" else dy).at[pl.ds(aligned(row0 + h * kr, kr), kr), :]
        return local(src, res.at[rs, :], s_res.at[h])

    def res_load(kind, h):
        def fn():
            res_copy(kind, h).start()

        return fn

    def g_stage(k, src, res_kind, hooks):
        pieces = LONG if k == 3 else SHORT
        count = len(pieces)

        def save(s):
            return local(gacc.at[s % 2], psm.at[k, pieces[s][1]], s_ps)

        def theirs(t):
            return [local(rc.at[k, t, rs], side.at[i], s_side.at[i]) for i, rs in enumerate((alpha, beta))]

        def send(t):
            if t == 0:
                x_msg(k, 0).start()
                y_msg(k, 0).start()
            elif t == 1:
                x_msg(k, 1).start()
            elif t == 2:
                y_msg(k, 1).start()

        hooks = {key: list(val) for key, val in hooks.items()}

        def first(s):
            def fn():
                if s >= 2 and pieces[s - 2][0] == "s":
                    c_msg(k, pieces[s - 2][1]).wait_send()
                if s >= 1:
                    if pieces[s - 1][0] == "s":
                        c_msg(k, pieces[s - 1][1]).start()
                    else:
                        save(s - 1).start()
                if pieces[s][0] == "m":
                    c_msg(k, pieces[s][1]).wait_recv()
                    for c in theirs(pieces[s][1]):
                        c.start()

            return fn

        def second(s):
            def fn():
                if s >= 1 and pieces[s - 1][0] == "m":
                    save(s - 1).wait()
                    send(pieces[s - 1][1])
                if pieces[s][0] == "m":
                    for c in theirs(pieces[s][1]):
                        c.wait()

            return fn

        for s in range(count):
            hooks.setdefault(2 * s, []).append(first(s))
            hooks.setdefault(2 * s + 1, []).append(second(s))
        if res_kind is not None:
            for h in range(2):
                hooks.setdefault(h, []).append(lambda h=h: res_copy(res_kind, h).wait())

        def body(u):
            @pl.when(u + 1 < 2 * count)
            def _():
                g_tile(k, src, u + 1).start()

            g_tile(k, src, u).wait()
            mine, _, xp, _ = piece_of(u // 2, count)
            again = u % 2
            slot = (u // 2) % 2
            for n in chunks:
                val = g_dot(k, u, xp, n)
                for i, rs in enumerate((slice(0, quart), slice(quart, half))):
                    more = gacc[slot, rs, n] + jnp.where(mine == 1, side[i + 2 * (1 - mine * again), :, n], 0.0)
                    gacc[slot, rs, n] = val[rs, :] + jnp.where(again == 1, more, 0.0)

        run_loop(2 * count, body, hooks)
        save(count - 1).start()
        save(count - 1).wait()
        send(pieces[count - 1][1])

    def last_tile(k, src, u):
        return tile_of(k, src, u, 0, xx, (1 - cc) + (u // 2) * (2 * cc - 1))

    def last_first(k, src, res_kind):
        def fn():
            res_load(res_kind, 0)()
            last_tile(k, src, 0).start()

        return fn

    def last_pieces(k, src, res_kind, hooks):
        res_load(res_kind, 1)()
        hooks = {key: list(val) for key, val in hooks.items()}
        for h in range(2):
            hooks.setdefault(h, []).append(lambda h=h: res_copy(res_kind, h).wait())
        hooks.setdefault(2, []).append(lambda: c_msg(k, 3).start())

        def body(u):
            @pl.when(u + 1 < 4)
            def _():
                last_tile(k, src, u + 1).start()

            last_tile(k, src, u).wait()
            slot = u // 2
            for n in chunks:
                gacc[slot, :, n] = g_dot(k, u, xx, n) + jnp.where(u % 2 == 1, gacc[slot, :, n], 0.0)

        run_loop(4, body, hooks)

    def sum_phases(k):
        def p0():
            for i in (1, 2):
                x_msg(k, i).wait_recv()
                y_msg(k, i).wait_recv()
            side_in(0, rx.at[k, 1]).start()
            side_in(1, ry.at[k, 2]).start()

        def p1():
            c_msg(k, 3).wait_send()
            c_msg(k, 3).wait_recv()
            side_in(2, rc.at[k, 3, alpha]).start()
            side_in(3, rc.at[k, 3, beta]).start()

        def p2():
            side_in(0, rx.at[k, 1]).wait()
            side_in(1, ry.at[k, 2]).wait()
            side_in(2, rc.at[k, 3, alpha]).wait()
            side_scale(0, (0, 1, 2), 0)
            side_out(0, gfin.at[k, alpha]).start()
            side_in(1, ry.at[k, 1]).start()
            side_in(2, rx.at[k, 2]).start()

        def p3():
            side_in(1, ry.at[k, 1]).wait()
            side_in(2, rx.at[k, 2]).wait()
            side_in(3, rc.at[k, 3, beta]).wait()
            side_scale(3, (1, 2, 3), quart)
            side_out(3, gfin.at[k, beta]).start()

        def p4():
            side_out(0, gfin.at[k, alpha]).wait()
            side_out(3, gfin.at[k, beta]).wait()
            if IS_UP[k]:
                to_sib(k).start()

        return p0, p1, p2, p3, p4

    nq = quart // 8

    def side_add(dst, a, b):
        side[dst] = side[a] + side[b]

    def side_scale(dst, parts, row=None):
        def f(i, acc):
            rs = pl.ds(aligned(i * 8, 8), 8)
            v = side[parts[0], rs, :]
            for p in parts[1:]:
                v = v + side[p, rs, :]
            if row is not None:
                v = v + gacc[1, pl.ds(aligned(row + i * 8, 8), 8), :]
            v = v * 0.25
            side[dst, rs, :] = v
            v = v * v
            for n in range(0, dim, 128):
                acc = acc + v[:, n:n + 128]
            return acc

        ss[...] = lax.fori_loop(0, nq, f, ss[...])

    def side_in(i, src):
        return local(src, side.at[i], s_side.at[i])

    def side_out(i, dst):
        return local(side.at[i], dst, s_side.at[i])

    def join_phases(k):
        ins = ((0, psm.at[k, 1, beta]), (1, ry.at[k, 0]), (2, psm.at[k, 2, alpha]), (3, rx.at[k, 0]))

        def pa():
            x_msg(k, 0).wait_recv()
            y_msg(k, 0).wait_recv()
            for i, s in ins:
                side_in(i, s).start()

        def pb():
            for i, s in ins:
                side_in(i, s).wait()
            side_add(0, 0, 1)
            side_add(2, 2, 3)
            side_out(0, x3.at[k, 0]).start()
            side_out(2, x3.at[k, 1]).start()

        def pc():
            side_out(0, x3.at[k, 0]).wait()
            side_out(2, x3.at[k, 1]).wait()
            x_msg(k, 2).start()
            y_msg(k, 2).start()

        return pa, pb, pc

    def to_sib(k):
        src = side.at[2 * (1 - cc)] if k == 3 else gfin.at[k, pl.ds(aligned((1 - cc) * quart, quart), quart), :]
        return remote(src, gsib.at[k // 2], f_snd.at[k // 2], f_rcv.at[k // 2], sib)

    def at(first, fns):
        return {first + i: [fn] for i, fn in enumerate(fns)}

    def merge(*tables):
        out = {}
        for table in tables:
            for key, fns in table.items():
                out.setdefault(key, []).extend(fns)
        return out

    w_load("u", 0, 0, 0)()
    for r in range(nz):
        x_copy(r).start()
    meet()
    for m in range(4):
        for sub in range(SUBS):
            w_y(m, sub).start()
    ss[...] = jnp.zeros_like(ss)

    w_wait("u", 0, 0, 0)()
    z_stage(1, 0, 0, z1, a1, merge(
        {4: [w_load("d", 0, 0, 1)]}, {10: [got_y(0, 0)]}, {15: [k_first(a1, 0)]}), wait_x=True)
    w_wait("d", 0, 0, 1)()
    k_stage(a1, 0, 1, False, None, merge(
        {1: [got_y(0, 1), got_x(0, 0)]}, {6: [got_y(1, 0), got_x(0, 1)]}, {7: [got_rest(0), w_load("u", 1, 0, 0)]}))
    w_wait("u", 1, 0, 0)()
    z_stage(1, 1, 0, z1, a1, merge(
        {4: [got_y(1, 1), got_x(1, 0)]},
        {12: [got_y(2, 0), got_x(1, 1), got_rest(1), w_load("d", 1, 0, 1)]}, {15: [k_first(a1, 1)]}))
    w_load("u", 0, 1, 0)()
    w_wait("d", 1, 0, 1)()
    k_stage(a1, 1, 1, False, hbuf, {3: [got_y(2, 1), got_x(2, 0)]})
    w_wait("u", 0, 1, 0)()
    z_stage(2, 0, 0, z3, a3, merge(
        {0: [got_y(3, 0), got_x(2, 1)]}, {9: [got_y(3, 1), got_x(3, 0)]},
        {11: [got_rest(2), w_load("u", 1, 1, 1)]}, {16: [w_wait("u", 1, 1, 1)]}, {20: [got_x(3, 1)]},
        {24: [res_load("dy", 0)]}, {31: [g_first(0, a3)]}), ending=(res_load("dy", 1),))
    g_stage(0, a3, "dy", merge(
        {3: [w_load("d", 0, 1, 0)]}, {5: [got_rest(3), w_load("d", 1, 1, 1)]}, {10: [q_first(z3)]}))
    w_wait("d", 0, 1, 0)()
    q_stage(z3, q3, merge(
        {16: [w_wait("d", 1, 1, 1)]}, at(8, join_phases(0)),
        {24: [res_load("h", 0)]}, {31: [g_first(1, q3)]}), ending=(res_load("h", 1),))
    g_stage(1, q3, "h", merge(
        {3: [w_load("u", 0, 1, 0)]}, {5: [w_load("u", 1, 1, 1)]}, {10: [k_first(q3, 0)]}))
    w_wait("u", 0, 1, 0)()
    k_stage(q3, 0, 0, True, None, at(5, join_phases(1)))
    k_first(q3, 1)()
    w_wait("u", 1, 1, 1)()
    k_stage(q3, 1, 1, True, ebuf, {nr - 1: [g_first(2, a1)]})
    g_stage(2, a1, None, merge(
        {3: [w_load("d", 0, 0, 0)]}, {5: [w_load("d", 1, 0, 1)]}, {10: [q_first(z1)]}))
    w_wait("d", 0, 0, 0)()
    q_stage(z1, q1, merge(
        {16: [w_wait("d", 1, 0, 1)]}, at(8, join_phases(2)),
        {24: [res_load("x", 0)]}, {31: [g_first(3, q1)]}), ending=(res_load("x", 1),))
    g_stage(3, q1, "x", {15: [last_first(0, a3, "dy")]})
    four, three, two = sum_phases(0), sum_phases(1), sum_phases(2)
    last_pieces(0, a3, "dy", {1: [four[0]], 3: [last_first(1, q3, "h")]})
    for fn in four[1:]:
        fn()
    for fn in join_phases(3):
        fn()
    last_pieces(1, q3, "h", {1: [three[0]], 3: [last_first(2, a1, "e")]})
    last_pieces(2, a1, "e", {0: [three[1]], 1: [three[2]], 2: [three[3]], 3: [three[4], two[0]]})
    for fn in two[1:]:
        fn()
    side_in(0, psm.at[3, 3, alpha]).start()
    side_in(2, psm.at[3, 3, beta]).start()
    x_msg(3, 1).wait_recv()
    side_in(1, rx.at[3, 1]).start()
    y_msg(3, 1).wait_recv()
    side_in(3, ry.at[3, 1]).start()
    side_in(0, psm.at[3, 3, alpha]).wait()
    side_in(1, rx.at[3, 1]).wait()
    side_add(0, 0, 1)
    side_in(2, psm.at[3, 3, beta]).wait()
    side_in(3, ry.at[3, 1]).wait()
    side_add(2, 2, 3)
    y_msg(3, 2).wait_recv()
    side_in(1, ry.at[3, 2]).start()
    x_msg(3, 2).wait_recv()
    side_in(3, rx.at[3, 2]).start()
    side_in(1, ry.at[3, 2]).wait()
    side_scale(0, (0, 1))
    side_out(0, gfin.at[3, alpha]).start()
    side_in(3, rx.at[3, 2]).wait()
    side_scale(2, (2, 3))
    side_out(2, gfin.at[3, beta]).start()
    to_sib(3).start()

    nbuf[me] = ss[...]

    def n_send(o):
        tid = (me + o) % 8
        return remote(ss, nbuf.at[me], n_snd.at[o], n_rcv.at[o], (tid // 4, tid % 4))

    def n_recv(o):
        return remote(ss, nbuf.at[(me + 8 - o) % 8], n_snd.at[o], n_rcv.at[o], sib)

    for o in range(1, 8):
        n_send(o).start()
    for o in range(1, 8):
        n_recv(o).wait_recv()
    acc = nbuf[0]
    for i in range(1, 8):
        acc = acc + nbuf[i]
    nrm[...] = acc

    side_out(0, gfin.at[3, alpha]).wait()
    side_out(2, gfin.at[3, beta]).wait()
    for k in (1, 3):
        to_sib(k).wait_recv()
        to_sib(k).wait_send()
    for o in range(1, 8):
        n_send(o).wait_send()
    for m in range(4):
        for sub in range(SUBS):
            for c in (w_y(m, sub), w_x(m, sub), w_c(m, sub), w_f(m, sub)):
                c.wait_send()
    for k in range(4):
        for i in range(3):
            x_msg(k, i).wait_send()
            y_msg(k, i).wait_send()


def gradients(act_in, grad_out, w_up, w_down):
    rows = act_in.shape[0] // 2
    dim = act_in.shape[1]
    wide = w_up.shape[2]
    half, quart = dim // 2, dim // 4
    bm, bz = rows // 8, rows // 16
    hbm = pltpu.HBM
    S = jax.ShapeDtypeStruct
    act = S((2, rows, wide), BF16)
    outs = [
        S((4, half, dim), F32), S((2, quart, dim), F32), S((8, 128), F32),
        S(w_up.shape, BF16), S(w_down.shape, BF16), act, act, act, act, act, act,
        S((rows, dim), BF16), S((rows, dim), BF16), S((rows, dim), F32),
        S((4, 4, half, dim), F32), S((4, 4, half, dim), F32),
        S((4, 3, quart, dim), F32), S((4, 3, quart, dim), F32), S((4, 2, quart, dim), F32),
    ]
    out_specs = [pl.BlockSpec(memory_space=hbm) for _ in outs]
    out_specs[2] = pl.BlockSpec(memory_space=pltpu.VMEM)
    dma = pltpu.SemaphoreType.DMA
    scratch = [
        pltpu.VMEM((4, dim, dim), BF16), pltpu.VMEM((4, bm, dim), BF16), pltpu.VMEM((2, half, dim), F32),
        pltpu.VMEM((8, bz, dim), BF16), pltpu.VMEM((rows, dim), BF16), pltpu.VMEM((2, rows // 2, dim), BF16),
        pltpu.VMEM((4, quart, dim), F32), pltpu.VMEM((8, 128), F32), pltpu.VMEM((8, 8, 128), F32),
        dma((16,)), dma((4,)), dma((4,)), dma((8,)), dma((2,)), dma, dma((2,)), dma((2,)), dma((4,)),
        dma((4, SUBS, 4)), dma((4, SUBS, 4)), dma((4, 10)), dma((4, 10)), dma((2,)), dma((2,)), dma((8,)), dma((8,)),
    ]
    flops = 20 * rows * dim * 2 * wide
    return pl.pallas_call(
        functools.partial(grad_kernel, rows, bm, bz, min(256, dim)),
        out_shape=outs,
        in_specs=[pl.BlockSpec(memory_space=hbm)] * 4,
        out_specs=out_specs,
        scratch_shapes=scratch,
        compiler_params=pltpu.CompilerParams(
            collective_id=0, has_side_effects=True, vmem_limit_bytes=66_900_000
        ),
        cost_estimate=pl.CostEstimate(flops=flops, bytes_accessed=1_500_000_000, transcendentals=0),
        name="grads",
    )(act_in, grad_out, w_up, w_down)[:3]


def update_kernel(is_up, where_ref, rate_ref, clip_ref, squares, *refs):
    grads, refs = refs[:1 + is_up], refs[1 + is_up:]
    master, mom, var = refs[:3]
    new_master, new_mom, new_var, wide, shard, scale = refs[-6:]
    cols = grads[0].shape[-1]

    @pl.when(pl.program_id(0) == 0)
    def _():
        norm = jnp.sqrt(jnp.sum(squares[...], keepdims=True))
        scale[...] = jnp.broadcast_to(jnp.minimum(1.0, clip_ref[0] / (norm + NORM_EPS)), scale.shape)

    clip_scale = scale[:1, :1]
    rate = rate_ref[0] / (1.0 - BETA_ONE ** STEP)
    for j in range(1 + is_up):
        cs = slice(j * cols, (j + 1) * cols)
        g = grads[0][0]
        if is_up:
            g = jnp.where(where_ref[1] == j, g, grads[1][0])
        scaled = clip_scale * g
        m = BETA_ONE * mom[0, :, cs] + (1.0 - BETA_ONE) * scaled
        v = BETA_TWO * var[0, :, cs] + ((1.0 - BETA_TWO) * scaled) * scaled
        new_mom[0, :, cs] = m
        new_var[0, :, cs] = v
        hat = v * (1.0 / (1.0 - BETA_TWO ** STEP))
        root = jnp.where(hat > 0.0, hat * lax.rsqrt(hat), 0.0)
        new = master[0, :, cs] - (rate * m) * pl.reciprocal(root + ADAM_EPS)
        new_master[0, :, cs] = new
        low = new.astype(BF16)
        wide[0, :, cs] = low
        shard[:, cs] = low


def update(is_up, k, mat, part, where, scalars, gfin, gsib, state, before):
    rows, cols = state[0].shape[1:]
    blocks = next(b for b in (5, 4, 2, 1) if rows % (32 * b) == 0)
    br = rows // (2 * blocks)
    skip = part * blocks
    dim = gfin.shape[2]

    def mine(i, w):
        return (mat, skip + i, 0)

    any_spec = pl.BlockSpec(memory_space=pl.ANY)
    state_spec = pl.BlockSpec((1, br, cols), mine)
    if is_up:
        g_specs = [pl.BlockSpec((1, br, dim), lambda i, w: (k, w[1] * 2 * blocks + skip + i, 0)), pl.BlockSpec((1, br, dim), lambda i, w: (k // 2, skip + i, 0))]
        g_args = [gfin, gsib]
    else:
        g_specs, g_args = [pl.BlockSpec((1, br, dim), lambda i, w: (k, skip + i, 0))], [gfin]
    held = list(before) if before is not None else []
    n_in = 4 + len(g_args) + 3
    smem = pl.BlockSpec(memory_space=pltpu.SMEM)
    S = jax.ShapeDtypeStruct
    shape = state[0].shape
    return pl.pallas_call(
        functools.partial(update_kernel, int(is_up)),
        out_shape=[S(shape, F32)] * 3 + [S((2, 4 * rows, cols), BF16), S((rows // 2, cols), BF16)],
        grid_spec=pltpu.PrefetchScalarGridSpec(
            num_scalar_prefetch=1, grid=(blocks,),
            in_specs=[smem, smem, pl.BlockSpec(memory_space=pltpu.VMEM)] + g_specs + [state_spec] * 3 + [any_spec] * len(held),
            out_specs=[state_spec] * 3 + [
                pl.BlockSpec((1, br, cols), lambda i, w: (mat, w[0] * 2 * blocks + skip + i, 0)), pl.BlockSpec((br, cols), lambda i, w: (i, 0))],
            scratch_shapes=[pltpu.VMEM((8, 128), F32)],
        ),
        input_output_aliases={n_in + i: i for i in range(len(held))},
        cost_estimate=pl.CostEstimate(flops=15 * rows * cols, bytes_accessed=16 * rows * cols, transcendentals=rows * cols),
        name="adam",
    )(where, *scalars, *g_args, *state, *held)


TO_FAR = [(0, 2), (2, 0), (1, 3), (3, 1)]
TO_SIB = [(0, 1), (1, 0), (2, 3), (3, 2)]


ORDER = [(up, k, mat, part) for up, k, mat in ((False, 2, 0), (False, 0, 1), (True, 3, 0), (True, 1, 1)) for part in (0, 1)]


def solution(mesh):
    spec_rows = P("data", None)
    spec_wup = P(None, None, "model")
    spec_wdown = P(None, "model", None)
    spec_sup = P(None, "data", "model")
    spec_sdown = P(None, ("model", "data"), None)
    spec_scalar = P(None)

    def local_step(act_in, grad_out, w_up, w_down, master_up, master_down, mom_up, mom_down, var_up, var_down, learn_rate, clip_norm):
        place = lax.axis_index("data")
        core = place % 2
        side = place // 2
        where = jnp.stack([place, core]).astype(jnp.int32)
        act_in, where = lax.optimization_barrier((act_in, where))
        gfin, gsib, squares = gradients(act_in, grad_out, w_up, w_down)
        norm_val = jnp.sqrt(jnp.sum(squares))
        scalars = (learn_rate, clip_norm, squares)
        state = {False: (master_down, mom_down, var_down), True: (master_up, mom_up, var_up)}
        done = {False: None, True: None}
        at_far, at_sib, at_diag = 2 * (1 - side) + core, 2 * side + 1 - core, 2 * (1 - side) + 1 - core

        def sib(shard):
            return lax.ppermute(shard, "data", TO_SIB)

        def put(is_up, mat, part, owner, piece):
            wide = done[is_up][3]
            start = owner * (wide.shape[1] // 4) + part * piece.shape[0]
            done[is_up][3] = lax.dynamic_update_slice(wide, piece[None], (mat, start, 0))

        sent = []
        for is_up, k, mat, part in ORDER:
            *done[is_up], shard = update(is_up, k, mat, part, where, scalars, gfin, gsib, state[is_up], done[is_up])
            where, shard = lax.optimization_barrier((where, shard))
            got = lax.ppermute(shard, "data", TO_FAR)
            sent.append((is_up, mat, part, shard, got))
        is_up, mat, part, shard, got = sent[0]
        put(is_up, mat, part, at_sib, sib(shard))
        late = None
        for i, (is_up, mat, part, shard, got) in enumerate(sent):
            got, done[True][3], done[False][3] = lax.optimization_barrier((got, done[True][3], done[False][3]))
            diag = sib(got)
            put(is_up, mat, part, at_far, got)
            if late is not None:
                put(*late)
            late = (is_up, mat, part, at_diag, diag)
            if i + 1 < len(sent):
                is_up, mat, part, shard, got = sent[i + 1]
                put(is_up, mat, part, at_sib, sib(shard))
        put(*late)
        up, down = done[True], done[False]
        new_w_up, new_w_down = up[3], down[3]
        return (new_w_up, new_w_down, up[0], down[0], up[1], down[1], up[2], down[2], norm_val.reshape(1))

    return jax.shard_map(local_step, mesh=mesh, in_specs=(spec_rows, spec_rows, spec_wup, spec_wdown, spec_sup, spec_sdown, spec_sup, spec_sdown, spec_sup, spec_sdown, spec_scalar, spec_scalar), out_specs=(spec_wup, spec_wdown, spec_sup, spec_sdown, spec_sup, spec_sdown, spec_sup, spec_sdown, spec_scalar), check_vma=False)
```

time: 1300 us -> 930 us (0.72)
  Pallas kernels: 1060 us -> 801 us
  waiting for transfers between devices: 153 us -> 80.7 us
  other arithmetic: 35 us -> 1.25 us
  between operations: 17.7 us -> 4.14 us
    pallas_call x1 -> x9, Pallas kernels: 1060 us -> 801 us  [the longest x1 736 us: gradients(): pl.pallas_call(functools.partial(grad_kernel, rows, bm, bz, min(256, dim)...]
    all_gather x2 -> x0, waiting for transfers between devices: 153 us -> none  [the longest x1 84.5 us: local_step(): lax.all_gather(new_master_down.astype(BF16), 'data', axis=1, tiled=True)]
    ppermute x0 -> x24, waiting for transfers between devices: none -> 80.7 us  [the longest x8 79.1 us: local_step(): got = lax.ppermute(shard, 'data', TO_FAR)]
    convert_element_type x2 -> x0, other arithmetic: 28.8 us -> none  [the longest x1 14.4 us: local_step(): new_master_up.astype(BF16)]
    dynamic_update_slice x0 -> x24, local copies, waits for them, and re-layouts: none -> 23.9 us  [put(): lax.dynamic_update_slice(wide, piece[None], (mat, start, 0))]
    unnamed x12 -> x8, local copies, waits for them, and re-layouts: 17.7 us -> 0.02 us
  transfers between devices with their start and end apart: 2 -> 24, of which waited for: 2 -> 8; matrix products, arithmetic and copies ran while one was open for 1% -> 3% of each run, Pallas kernels for 0% -> 6%
where the time goes in v2:
time: 930 us; the launch traced here: 921 us
  Pallas kernels  801 us (86%)
  waiting for transfers between devices  80.7 us (9%)
  local copies, waits for them, and re-layouts  24 us (3%)
  starting transfers between devices  9.72 us (1%)
    pallas_call x1, Pallas kernels, gradients(): pl.pallas_call(functools.partial(grad_kernel, rows, bm, bz, min(256, dim)...  736 us
    ppermute x8, waiting for transfers between devices, local_step(): got = lax.ppermute(shard, 'data', TO_FAR)  79.1 us
    pallas_call x8, Pallas kernels, update(): pl.pallas_call(functools.partial(update_kernel, int(is_up)), out_shape=[S...  65.5 us
    dynamic_update_slice x24, local copies, waits for them, and re-layouts, put(): lax.dynamic_update_slice(wide, piece[None], (mat, start, 0))  23.9 us
  transfers between devices with their start and end apart: 24, of which 8 were waited for; matrix products, arithmetic and copies ran while one was open for 3% of the time, Pallas kernels for 6%

profile of v2, /device:TPU:0, one launch (start us, length us, event | category | flops | bytes accessed | tf_op | source)
XLA Modules:
  0.0 921.1 jit_solution(16705999345570502570)
XLA Ops:
  0.7 0.7 pad_add_fusion.where_ref
  2.6 735.8 %grads.1 = (f32[4,640,1280]{2,1,0:T(8,128)}, f32[2,320,1280]{2,1,0:T(8,128)}, f32[8,128]{1,0:T(8,128)}, bf16[2,1280,2560]{2,1,0:T(8,128)(2,1)}, bf16[2,2560,1280...) custom-call(bf16[8192,1280]{1,0:T(8,128)(2,1)} %x, ...), custom_call_target="tpu_custom_call" | custom-call | flops 536870912000 | bytes 1500000000 | tf_op jit(solution)/shard_map/grads/pallas_call | solution.py:796
  738.4 8.2 adam.8
  746.6 0.4 collective-permute-start.8
  747.0 0.5 collective-permute-start.7
  747.6 8.2 adam.9
  755.8 0.0 collective-permute-start.9
  755.8 1.5 collective-permute-start.6
  757.3 8.2 adam.10
  765.5 0.2 collective-permute-start.11
  765.7 8.2 adam.11
  773.9 8.2 adam.12
  782.1 8.1 adam.13
  790.3 8.1 adam.14
  798.4 8.1 adam.15
  806.6 0.6 reduce_sum.9
  808.0 0.0 collective-permute-done.8
  808.0 0.5 collective-permute-start.5
  808.6 2.2 bitcast_dynamic-update-slice_fusion.23
  810.8 0.0 collective-permute-start.13
  810.8 0.9 bitcast_dynamic-update-slice_fusion.22
  811.8 0.0 collective-permute-done.9
  811.8 0.5 collective-permute-start.10
  812.3 0.9 bitcast_dynamic-update-slice_fusion.21
  813.2 0.0 collective-permute-done.6
  813.2 1.3 collective-permute-start.4
  814.6 0.9 bitcast_dynamic-update-slice_fusion.20
  815.5 0.9 bitcast_dynamic-update-slice_fusion.19
  816.4 0.0 collective-permute-done.11
  816.5 0.5 collective-permute-start.12
  817.0 0.9 bitcast_dynamic-update-slice_fusion.18
  817.9 11.5 %collective-permute-done.5 = bf16[320,1280]{1,0:T(8,128)(2,1)S(1)} collective-permute-done((bf16[320,1280]{1,0:T(8,128)(2,1)}, bf16[320,1280]{1,0:T(8,128)(2,1)S(1)}, u32[]{:S(2)}, u32[]{:S(2)}) %collective-permute-start.5) | collective-permute-done | bytes 819232 | tf_op jit(solution)/shard_map/ppermute | solution.py:920
  829.4 0.5 collective-permute-start.3
  829.9 0.9 bitcast_dynamic-update-slice_fusion.17
  830.8 0.9 bitcast_dynamic-update-slice_fusion.16
  831.8 1.5 collective-permute-start.2
  833.3 0.9 bitcast_dynamic-update-slice_fusion.15
  834.2 12.7 %collective-permute-done.4 = bf16[320,1280]{1,0:T(8,128)(2,1)S(1)} collective-permute-done((bf16[320,1280]{1,0:T(8,128)(2,1)}, bf16[320,1280]{1,0:T(8,128)(2,1)S(1)}, u32[]{:S(2)}, u32[]{:S(2)}) %collective-permute-start.4) | collective-permute-done | bytes 819232 | tf_op jit(solution)/shard_map/ppermute | solution.py:920
  846.9 0.5 collective-permute-start.15
  847.4 0.9 bitcast_dynamic-update-slice_fusion.14
  848.4 0.9 bitcast_dynamic-update-slice_fusion.13
  849.3 1.1 collective-permute-done.15
  850.4 0.5 collective-permute-start.1
  850.9 0.9 bitcast_dynamic-update-slice_fusion.12
  851.9 12.6 %collective-permute-done.3 = bf16[160,2560]{1,0:T(8,128)(2,1)S(1)} collective-permute-done((bf16[160,2560]{1,0:T(8,128)(2,1)}, bf16[160,2560]{1,0:T(8,128)(2,1)S(1)}, u32[]{:S(2)}, u32[]{:S(2)}) %collective-permute-start.3) | collective-permute-done | bytes 819232 | tf_op jit(solution)/shard_map/ppermute | solution.py:920
  864.5 0.9 bitcast_dynamic-update-slice_fusion.11
  865.4 0.5 collective-permute-start.21
  865.9 0.9 bitcast_dynamic-update-slice_fusion.10
  866.9 0.1 collective-permute-start.18
  866.9 0.9 bitcast_dynamic-update-slice_fusion.9
  867.9 14.1 %collective-permute-done.2 = bf16[160,2560]{1,0:T(8,128)(2,1)S(1)} collective-permute-done((bf16[160,2560]{1,0:T(8,128)(2,1)S(1)}, bf16[160,2560]{1,0:T(8,128)(2,1)S(1)}, u32[]{:S(2)}, u32[]{:S(2)}) %collective-permute-start.2) | collective-permute-done | bytes 819232 | tf_op jit(solution)/shard_map/ppermute | solution.py:920
  882.0 0.5 collective-permute-start
  882.5 0.9 bitcast_dynamic-update-slice_fusion.8
  883.5 0.9 bitcast_dynamic-update-slice_fusion.7
  884.4 0.9 bitcast_dynamic-update-slice_fusion.6
  885.4 14.2 %collective-permute-done.1 = bf16[160,2560]{1,0:T(8,128)(2,1)S(1)} collective-permute-done((bf16[160,2560]{1,0:T(8,128)(2,1)S(1)}, bf16[160,2560]{1,0:T(8,128)(2,1)S(1)}, u32[]{:S(2)}, u32[]{:S(2)}) %collective-permute-start.1) | collective-permute-done | bytes 819232 | tf_op jit(solution)/shard_map/ppermute | solution.py:920
  899.6 0.9 bitcast_dynamic-update-slice_fusion.5
  900.5 0.9 bitcast_dynamic-update-slice_fusion.4
  901.5 0.9 bitcast_dynamic-update-slice_fusion.3
  902.4 14.1 %collective-permute-done = bf16[160,2560]{1,0:T(8,128)(2,1)S(1)} collective-permute-done((bf16[160,2560]{1,0:T(8,128)(2,1)S(1)}, bf16[160,2560]{1,0:T(8,128)(2,1)S(1)}, u32[]{:S(2)}, u32[]{:S(2)}) %collective-permute-start) | collective-permute-done | bytes 819232 | tf_op jit(solution)/shard_map/ppermute | solution.py:920
  916.5 0.9 bitcast_dynamic-update-slice_fusion.2
  917.4 0.9 bitcast_dynamic-update-slice_fusion.1
  918.4 0.4 collective-permute-done.23
  918.8 0.9 bitcast_dynamic-update-slice_fusion
  (27 shorter events, 0.1 us)
Async XLA Ops:
  746.6 61.4 %collective-permute-start.8 = (bf16[320,1280]{1,0:T(8,128)(2,1)}, bf16[320,1280]{1,0:T(8,128)(2,1)}, u32[]{:S(2)}, u32[]{:S(2)}) collective-permute-start(bf16[320,1280]{1,0:T(8,128)(2,1)} %get-tuple-element.144), channel_id=1, source_target_pairs={{0,1},{1,0},{2,3},{3,2},{4,5},{5,4},{6,7},{7,6}} | collective-permute-start | bytes 2457608 | tf_op jit(solution)/shard_map/ppermute | solution.py:909
  747.0 63.8 %collective-permute-start.7 = (bf16[320,1280]{1,0:T(8,128)(2,1)}, bf16[320,1280]{1,0:T(8,128)(2,1)S(1)}, u32[]{:S(2)}, u32[]{:S(2)}) collective-permute-start(bf16[320,1280]{1,0:T(8,128)(2,1)} %get-tuple-element.144), channel_id=1, source_target_pairs={{0,2},{2,0},{1,3},{3,1},{4,6},{6,4},{5,7},{7,5}} | collective-permute-start | bytes 2457608 | tf_op jit(solution)/shard_map/ppermute | solution.py:920
  755.8 56.0 %collective-permute-start.9 = (bf16[320,1280]{1,0:T(8,128)(2,1)}, bf16[320,1280]{1,0:T(8,128)(2,1)S(1)}, u32[]{:S(2)}, u32[]{:S(2)}) collective-permute-start(bf16[320,1280]{1,0:T(8,128)(2,1)} %get-tuple-element.143), channel_id=1, source_target_pairs={{0,1},{1,0},{2,3},{3,2},{4,5},{5,4},{6,7},{7,6}} | collective-permute-start | bytes 2457608 | tf_op jit(solution)/shard_map/ppermute | solution.py:909
  755.8 57.4 %collective-permute-start.6 = (bf16[320,1280]{1,0:T(8,128)(2,1)}, bf16[320,1280]{1,0:T(8,128)(2,1)S(1)}, u32[]{:S(2)}, u32[]{:S(2)}) collective-permute-start(bf16[320,1280]{1,0:T(8,128)(2,1)} %get-tuple-element.143), channel_id=1, source_target_pairs={{0,2},{2,0},{1,3},{3,1},{4,6},{6,4},{5,7},{7,5}} | collective-permute-start | bytes 2457608 | tf_op jit(solution)/shard_map/ppermute | solution.py:920
  765.5 50.9 %collective-permute-start.11 = (bf16[320,1280]{1,0:T(8,128)(2,1)}, bf16[320,1280]{1,0:T(8,128)(2,1)S(1)}, u32[]{:S(2)}, u32[]{:S(2)}) collective-permute-start(bf16[320,1280]{1,0:T(8,128)(2,1)} %get-tuple-element.142), channel_id=1, source_target_pairs={{0,1},{1,0},{2,3},{3,2},{4,5},{5,4},{6,7},{7,6}} | collective-permute-start | bytes 2457608 | tf_op jit(solution)/shard_map/ppermute | solution.py:909
  798.4 8.2 copy-start
  808.0 23.8 %copy-start.3 = (bf16[160,2560]{1,0:T(8,128)(2,1)S(1)}, bf16[160,2560]{1,0:T(8,128)(2,1)}, u32[]{:S(2)}) copy-start(bf16[160,2560]{1,0:T(8,128)(2,1)} %get-tuple-element.139) | copy-start | bytes 2457604
  808.0 38.9 %copy-start.2 = (bf16[160,2560]{1,0:T(8,128)(2,1)S(1)}, bf16[160,2560]{1,0:T(8,128)(2,1)}, u32[]{:S(2)}) copy-start(bf16[160,2560]{1,0:T(8,128)(2,1)} %get-tuple-element.138) | copy-start | bytes 2457604
  808.0 57.4 %copy-start.1 = (bf16[160,2560]{1,0:T(8,128)(2,1)S(1)}, bf16[160,2560]{1,0:T(8,128)(2,1)}, u32[]{:S(2)}) copy-start(bf16[160,2560]{1,0:T(8,128)(2,1)} %get-tuple-element.137) | copy-start | bytes 2457604
  808.0 21.3 %collective-permute-start.5 = (bf16[320,1280]{1,0:T(8,128)(2,1)}, bf16[320,1280]{1,0:T(8,128)(2,1)S(1)}, u32[]{:S(2)}, u32[]{:S(2)}) collective-permute-start(bf16[320,1280]{1,0:T(8,128)(2,1)} %get-tuple-element.142), channel_id=1, source_target_pairs={{0,2},{2,0},{1,3},{3,1},{4,6},{6,4},{5,7},{7,5}} | collective-permute-start | bytes 2457608 | tf_op jit(solution)/shard_map/ppermute | solution.py:920
  810.8 21.0 %collective-permute-start.13 = (bf16[320,1280]{1,0:T(8,128)(2,1)}, bf16[320,1280]{1,0:T(8,128)(2,1)S(1)}, u32[]{:S(2)}, u32[]{:S(2)}) collective-permute-start(bf16[320,1280]{1,0:T(8,128)(2,1)} %get-tuple-element.141), channel_id=1, source_target_pairs={{0,1},{1,0},{2,3},{3,2},{4,5},{5,4},{6,7},{7,6}} | collective-permute-start | bytes 2457608 | tf_op jit(solution)/shard_map/ppermute | solution.py:909
  811.8 3.7 collective-permute-start.10
  813.2 33.7 %collective-permute-start.4 = (bf16[320,1280]{1,0:T(8,128)(2,1)}, bf16[320,1280]{1,0:T(8,128)(2,1)S(1)}, u32[]{:S(2)}, u32[]{:S(2)}) collective-permute-start(bf16[320,1280]{1,0:T(8,128)(2,1)} %get-tuple-element.141), channel_id=1, source_target_pairs={{0,2},{2,0},{1,3},{3,1},{4,6},{6,4},{5,7},{7,5}} | collective-permute-start | bytes 2457608 | tf_op jit(solution)/shard_map/ppermute | solution.py:920
  815.5 31.4 %collective-permute-start.14 = (bf16[160,2560]{1,0:T(8,128)(2,1)}, bf16[160,2560]{1,0:T(8,128)(2,1)S(1)}, u32[]{:S(2)}, u32[]{:S(2)}) collective-permute-start(bf16[160,2560]{1,0:T(8,128)(2,1)} %get-tuple-element.140), channel_id=1, source_target_pairs={{0,1},{1,0},{2,3},{3,2},{4,5},{5,4},{6,7},{7,6}} | collective-permute-start | bytes 2457608 | tf_op jit(solution)/shard_map/ppermute | solution.py:909
  816.5 14.4 %collective-permute-start.12 = (bf16[320,1280]{1,0:T(8,128)(2,1)S(1)}, bf16[320,1280]{1,0:T(8,128)(2,1)S(1)}, u32[]{:S(2)}, u32[]{:S(2)}) collective-permute-start(bf16[320,1280]{1,0:T(8,128)(2,1)S(1)} %collective-permute-done.6), channel_id=1, source_target_pairs={{0,1},{1,0},{2,3},{3,2},{4,5},{5,4},{6,7},{7,6}} | collective-permute-start | bytes 2457608 | tf_op jit(solution)/shard_map/ppermute | solution.py:909
  829.4 35.1 %collective-permute-start.3 = (bf16[160,2560]{1,0:T(8,128)(2,1)}, bf16[160,2560]{1,0:T(8,128)(2,1)S(1)}, u32[]{:S(2)}, u32[]{:S(2)}) collective-permute-start(bf16[160,2560]{1,0:T(8,128)(2,1)} %get-tuple-element.140), channel_id=1, source_target_pairs={{0,2},{2,0},{1,3},{3,1},{4,6},{6,4},{5,7},{7,5}} | collective-permute-start | bytes 2457608 | tf_op jit(solution)/shard_map/ppermute | solution.py:920
  830.8 34.6 %collective-permute-start.16 = (bf16[160,2560]{1,0:T(8,128)(2,1)}, bf16[160,2560]{1,0:T(8,128)(2,1)S(1)}, u32[]{:S(2)}, u32[]{:S(2)}) collective-permute-start(bf16[160,2560]{1,0:T(8,128)(2,1)} %get-tuple-element.139), channel_id=1, source_target_pairs={{0,1},{1,0},{2,3},{3,2},{4,5},{5,4},{6,7},{7,6}} | collective-permute-start | bytes 2457608 | tf_op jit(solution)/shard_map/ppermute | solution.py:909
  831.8 50.2 %collective-permute-start.2 = (bf16[160,2560]{1,0:T(8,128)(2,1)S(1)}, bf16[160,2560]{1,0:T(8,128)(2,1)S(1)}, u32[]{:S(2)}, u32[]{:S(2)}) collective-permute-start(bf16[160,2560]{1,0:T(8,128)(2,1)S(1)} %copy-done.3), channel_id=1, source_target_pairs={{0,2},{2,0},{1,3},{3,1},{4,6},{6,4},{5,7},{7,5}} | collective-permute-start | bytes 2457608 | tf_op jit(solution)/shard_map/ppermute | solution.py:920
  846.9 37.5 %collective-permute-start.19 = (bf16[160,2560]{1,0:T(8,128)(2,1)S(1)}, bf16[160,2560]{1,0:T(8,128)(2,1)S(1)}, u32[]{:S(2)}, u32[]{:S(2)}) collective-permute-start(bf16[160,2560]{1,0:T(8,128)(2,1)S(1)} %copy-done.2), channel_id=1, source_target_pairs={{0,1},{1,0},{2,3},{3,2},{4,5},{5,4},{6,7},{7,6}} | collective-permute-start | bytes 2457608 | tf_op jit(solution)/shard_map/ppermute | solution.py:909
  846.9 3.5 collective-permute-start.15
  850.4 49.2 %collective-permute-start.1 = (bf16[160,2560]{1,0:T(8,128)(2,1)S(1)}, bf16[160,2560]{1,0:T(8,128)(2,1)S(1)}, u32[]{:S(2)}, u32[]{:S(2)}) collective-permute-start(bf16[160,2560]{1,0:T(8,128)(2,1)S(1)} %copy-done.2), channel_id=1, source_target_pairs={{0,2},{2,0},{1,3},{3,1},{4,6},{6,4},{5,7},{7,5}} | collective-permute-start | bytes 2457608 | tf_op jit(solution)/shard_map/ppermute | solution.py:920
  864.5 2.4 collective-permute-start.17
  865.4 36.1 %collective-permute-start.21 = (bf16[160,2560]{1,0:T(8,128)(2,1)S(1)}, bf16[160,2560]{1,0:T(8,128)(2,1)S(1)}, u32[]{:S(2)}, u32[]{:S(2)}) collective-permute-start(bf16[160,2560]{1,0:T(8,128)(2,1)S(1)} %copy-done.1), channel_id=1, source_target_pairs={{0,1},{1,0},{2,3},{3,2},{4,5},{5,4},{6,7},{7,6}} | collective-permute-start | bytes 2457608 | tf_op jit(solution)/shard_map/ppermute | solution.py:909
  866.9 16.6 %collective-permute-start.18 = (bf16[160,2560]{1,0:T(8,128)(2,1)S(1)}, bf16[160,2560]{1,0:T(8,128)(2,1)S(1)}, u32[]{:S(2)}, u32[]{:S(2)}) collective-permute-start(bf16[160,2560]{1,0:T(8,128)(2,1)S(1)} %collective-permute-done.3), channel_id=1, source_target_pairs={{0,1},{1,0},{2,3},{3,2},{4,5},{5,4},{6,7},{7,6}} | collective-permute-start | bytes 2457608 | tf_op jit(solution)/shard_map/ppermute | solution.py:909
  882.0 34.5 %collective-permute-start = (bf16[160,2560]{1,0:T(8,128)(2,1)S(1)}, bf16[160,2560]{1,0:T(8,128)(2,1)S(1)}, u32[]{:S(2)}, u32[]{:S(2)}) collective-permute-start(bf16[160,2560]{1,0:T(8,128)(2,1)S(1)} %copy-done.1), channel_id=1, source_target_pairs={{0,2},{2,0},{1,3},{3,1},{4,6},{6,4},{5,7},{7,5}} | collective-permute-start | bytes 2457608 | tf_op jit(solution)/shard_map/ppermute | solution.py:920
  883.5 17.0 %collective-permute-start.20 = (bf16[160,2560]{1,0:T(8,128)(2,1)S(1)}, bf16[160,2560]{1,0:T(8,128)(2,1)S(1)}, u32[]{:S(2)}, u32[]{:S(2)}) collective-permute-start(bf16[160,2560]{1,0:T(8,128)(2,1)S(1)} %collective-permute-done.2), channel_id=1, source_target_pairs={{0,1},{1,0},{2,3},{3,2},{4,5},{5,4},{6,7},{7,6}} | collective-permute-start | bytes 2457608 | tf_op jit(solution)/shard_map/ppermute | solution.py:909
  899.6 17.9 %collective-permute-start.22 = (bf16[160,2560]{1,0:T(8,128)(2,1)S(1)}, bf16[160,2560]{1,0:T(8,128)(2,1)S(1)}, u32[]{:S(2)}, u32[]{:S(2)}) collective-permute-start(bf16[160,2560]{1,0:T(8,128)(2,1)S(1)} %collective-permute-done.1), channel_id=1, source_target_pairs={{0,1},{1,0},{2,3},{3,2},{4,5},{5,4},{6,7},{7,6}} | collective-permute-start | bytes 2457608 | tf_op jit(solution)/shard_map/ppermute | solution.py:909
  916.5 2.3 collective-permute-start.23

commit v3 on v2

--- a/solution.py
+++ b/solution.py
@@ -19,8 +19,9 @@
 GELU_ONE = 0.7978845608028654
 GELU_TWO = GELU_ONE * 0.044715
 IS_UP = (False, True, False, True)
-LONG = (("s", 0), ("s", 1), ("m", 0), ("s", 2), ("m", 1), ("s", 3), ("m", 2), ("m", 3))
-SHORT = (("s", 0), ("s", 1), ("m", 0), ("s", 2), ("m", 1), ("m", 2))
+SOON = (("s", 0), ("m", 0), ("s", 1), ("s", 2), ("m", 1), ("m", 2))
+EVEN = (("s", 0), ("s", 1), ("m", 0), ("s", 2), ("m", 1), ("m", 2))
+ORDERS = (EVEN, EVEN, EVEN, SOON)
 SUBS = 2
 
 
@@ -50,7 +51,7 @@
 def grad_kernel(
     rows, bm, bz, nc,
     x, dy, wu, wd,
-    gfin, gsib, nrm, wou, wod, z1, a1, z3, a3, q3, q1, hbuf, ebuf, hpart, psm, rc, rx, ry, x3,
+    gfin, gsib, nrm, where, wou, wod, z1, a1, z3, a3, q3, q1, hbuf, ebuf, hpart, psm, rc, rx, ry, x3,
     wb, ring, gacc, outs, res, gs, side, ss, nbuf,
     s_x, s_w, s_ring, s_out, s_gacc, s_ps, s_res, s_gs, s_side,
     w_snd, w_rcv, g_snd, g_rcv, f_snd, f_rcv, n_snd, n_rcv,
@@ -91,6 +92,9 @@
             pl.semaphore_signal(barrier, inc=1, device_id=(tid // 4, tid % 4), device_id_type=MESH)
         pl.semaphore_wait(barrier, 7)
 
+    where[0] = dd
+    where[1] = cc
+
     mats = ((wu, wou, 0), (wd, wod, 0), (wu, wou, 1), (wd, wod, 1))
 
     def chunk(ref, m, q, sub):
@@ -385,7 +389,7 @@
     alpha, beta = pl.ds(0, quart), pl.ds(quart, quart)
 
     def c_msg(k, t):
-        slot = (LONG if k == 3 else SHORT).index(("s", t)) % 2 if k == 3 or t < 3 else 0
+        slot = ORDERS[k].index(("s", t)) % 2 if t < 3 else 0
         return remote(gacc.at[slot], rc.at[k, t], g_snd.at[k, t], g_rcv.at[k, t], sib)
 
     def x_msg(k, i):
@@ -396,8 +400,10 @@
         src = (psm.at[k, 0, beta], psm.at[k, 2, beta], x3.at[k, 1])[i]
         return remote(src, ry.at[k, i], g_snd.at[k, 7 + i], g_rcv.at[k, 7 + i], ynb)
 
-    def piece_of(s, count):
-        v = s + s // (count - 1)
+    def piece_of(s, k):
+        if k == 3:
+            s = s + ((s + 6) // 7) * ((8 - s) // 7) - ((s + 5) // 7) * ((9 - s) // 7)
+        v = s + s // 5
         mine = (1 - v % 2) * ((v + 7) // 8)
         t = mine * (v // 2 - 1) + (1 - mine) * ((v + 1) // 2)
         oth = 1 - t % 2
@@ -412,7 +418,7 @@
         return local(src.at[oth, krow, col], gs.at[u % 2, :, pl.ds(0, half)], s_gs.at[u % 2])
 
     def g_tile(k, src, u):
-        _, oth, xp, cp = piece_of(u // 2, 8 if k == 3 else 6)
+        _, oth, xp, cp = piece_of(u // 2, k)
         return tile_of(k, src, u, oth, xp, cp)
 
     def g_first(k, src):
@@ -442,7 +448,7 @@
         return fn
 
     def g_stage(k, src, res_kind, hooks):
-        pieces = LONG if k == 3 else SHORT
+        pieces = ORDERS[k]
         count = len(pieces)
 
         def save(s):
@@ -471,7 +477,10 @@
                         c_msg(k, pieces[s - 1][1]).start()
                     else:
                         save(s - 1).start()
-                if pieces[s][0] == "m":
+                        if k == 3 and pieces[s - 1][1] == 0:
+                            save(s - 1).wait()
+                            send(0)
+                if pieces[s][0] == "m" and not (k == 3 and s == 1):
                     c_msg(k, pieces[s][1]).wait_recv()
                     for c in theirs(pieces[s][1]):
                         c.start()
@@ -480,9 +489,13 @@
 
         def second(s):
             def fn():
-                if s >= 1 and pieces[s - 1][0] == "m":
+                if s >= 1 and pieces[s - 1][0] == "m" and not (k == 3 and pieces[s - 1][1] == 0):
                     save(s - 1).wait()
                     send(pieces[s - 1][1])
+                if k == 3 and s == 1:
+                    c_msg(k, pieces[s][1]).wait_recv()
+                    for c in theirs(pieces[s][1]):
+                        c.start()
                 if pieces[s][0] == "m":
                     for c in theirs(pieces[s][1]):
                         c.wait()
@@ -502,7 +515,7 @@
                 g_tile(k, src, u + 1).start()
 
             g_tile(k, src, u).wait()
-            mine, _, xp, _ = piece_of(u // 2, count)
+            mine, _, xp, _ = piece_of(u // 2, k)
             again = u % 2
             slot = (u // 2) % 2
             for n in chunks:
@@ -661,14 +674,14 @@
 
     w_wait("u", 0, 0, 0)()
     z_stage(1, 0, 0, z1, a1, merge(
-        {4: [w_load("d", 0, 0, 1)]}, {10: [got_y(0, 0)]}, {15: [k_first(a1, 0)]}), wait_x=True)
+        {4: [w_load("d", 0, 0, 1)]}, {9: [got_y(0, 0)]}, {15: [k_first(a1, 0)]}), wait_x=True)
     w_wait("d", 0, 0, 1)()
     k_stage(a1, 0, 1, False, None, merge(
         {1: [got_y(0, 1), got_x(0, 0)]}, {6: [got_y(1, 0), got_x(0, 1)]}, {7: [got_rest(0), w_load("u", 1, 0, 0)]}))
     w_wait("u", 1, 0, 0)()
     z_stage(1, 1, 0, z1, a1, merge(
-        {4: [got_y(1, 1), got_x(1, 0)]},
-        {12: [got_y(2, 0), got_x(1, 1), got_rest(1), w_load("d", 1, 0, 1)]}, {15: [k_first(a1, 1)]}))
+        {3: [got_y(1, 1)]}, {6: [got_x(1, 0)]}, {9: [got_y(2, 0)]},
+        {14: [got_x(1, 1)]}, {15: [k_first(a1, 1), got_rest(1), w_load("d", 1, 0, 1)]}))
     w_load("u", 0, 1, 0)()
     w_wait("d", 1, 0, 1)()
     k_stage(a1, 1, 1, False, hbuf, {3: [got_y(2, 1), got_x(2, 0)]})
@@ -696,38 +709,40 @@
     q_stage(z1, q1, merge(
         {16: [w_wait("d", 1, 0, 1)]}, at(8, join_phases(2)),
         {24: [res_load("x", 0)]}, {31: [g_first(3, q1)]}), ending=(res_load("x", 1),))
-    g_stage(3, q1, "x", {15: [last_first(0, a3, "dy")]})
+    g_stage(3, q1, "x", {11: [last_first(0, a3, "dy")]})
     four, three, two = sum_phases(0), sum_phases(1), sum_phases(2)
-    last_pieces(0, a3, "dy", {1: [four[0]], 3: [last_first(1, q3, "h")]})
-    for fn in four[1:]:
-        fn()
+
+    def one_in():
+        x_msg(3, 1).wait_recv()
+        y_msg(3, 1).wait_recv()
+        side_in(0, rx.at[3, 1]).start()
+        side_in(2, ry.at[3, 1]).start()
+
+    last_pieces(0, a3, "dy", {3: [last_first(1, q3, "h")]})
     for fn in join_phases(3):
         fn()
-    last_pieces(1, q3, "h", {1: [three[0]], 3: [last_first(2, a1, "e")]})
-    last_pieces(2, a1, "e", {0: [three[1]], 1: [three[2]], 2: [three[3]], 3: [three[4], two[0]]})
-    for fn in two[1:]:
-        fn()
-    side_in(0, psm.at[3, 3, alpha]).start()
-    side_in(2, psm.at[3, 3, beta]).start()
-    x_msg(3, 1).wait_recv()
-    side_in(1, rx.at[3, 1]).start()
-    y_msg(3, 1).wait_recv()
-    side_in(3, ry.at[3, 1]).start()
-    side_in(0, psm.at[3, 3, alpha]).wait()
-    side_in(1, rx.at[3, 1]).wait()
+    last_pieces(1, q3, "h", {0: [four[0], four[1]], 1: [four[2]], 2: [four[3]], 3: [four[4], last_first(2, a1, "e"), three[0]]})
+    last_pieces(2, a1, "e", {0: [three[1]], 1: [three[2]], 2: [three[3]], 3: [three[4], last_first(3, q1, "x"), two[0]]})
+    last_pieces(3, q1, "x", {0: [two[1]], 1: [two[2]], 2: [two[3]], 3: [two[4], one_in]})
+    c_msg(3, 3).wait_send()
+    c_msg(3, 3).wait_recv()
+    side_in(1, rc.at[3, 3, alpha]).start()
+    side_in(3, rc.at[3, 3, beta]).start()
+    side_in(0, rx.at[3, 1]).wait()
+    side_in(2, ry.at[3, 1]).wait()
+    side_in(1, rc.at[3, 3, alpha]).wait()
     side_add(0, 0, 1)
-    side_in(2, psm.at[3, 3, beta]).wait()
-    side_in(3, ry.at[3, 1]).wait()
+    side_in(3, rc.at[3, 3, beta]).wait()
     side_add(2, 2, 3)
     y_msg(3, 2).wait_recv()
     side_in(1, ry.at[3, 2]).start()
     x_msg(3, 2).wait_recv()
     side_in(3, rx.at[3, 2]).start()
     side_in(1, ry.at[3, 2]).wait()
-    side_scale(0, (0, 1))
+    side_scale(0, (0, 1), 0)
     side_out(0, gfin.at[3, alpha]).start()
     side_in(3, rx.at[3, 2]).wait()
-    side_scale(2, (2, 3))
+    side_scale(2, (2, 3), quart)
     side_out(2, gfin.at[3, beta]).start()
     to_sib(3).start()
 
@@ -776,7 +791,7 @@
     S = jax.ShapeDtypeStruct
     act = S((2, rows, wide), BF16)
     outs = [
-        S((4, half, dim), F32), S((2, quart, dim), F32), S((8, 128), F32),
+        S((4, half, dim), F32), S((2, quart, dim), F32), S((8, 128), F32), S((2,), jnp.int32),
         S(w_up.shape, BF16), S(w_down.shape, BF16), act, act, act, act, act, act,
         S((rows, dim), BF16), S((rows, dim), BF16), S((rows, dim), F32),
         S((4, 4, half, dim), F32), S((4, 4, half, dim), F32),
@@ -784,6 +799,7 @@
     ]
     out_specs = [pl.BlockSpec(memory_space=hbm) for _ in outs]
     out_specs[2] = pl.BlockSpec(memory_space=pltpu.VMEM)
+    out_specs[3] = pl.BlockSpec(memory_space=pltpu.SMEM)
     dma = pltpu.SemaphoreType.DMA
     scratch = [
         pltpu.VMEM((4, dim, dim), BF16), pltpu.VMEM((4, bm, dim), BF16), pltpu.VMEM((2, half, dim), F32),
@@ -804,7 +820,7 @@
         ),
         cost_estimate=pl.CostEstimate(flops=flops, bytes_accessed=1_500_000_000, transcendentals=0),
         name="grads",
-    )(act_in, grad_out, w_up, w_down)[:3]
+    )(act_in, grad_out, w_up, w_down)[:4]
 
 
 def update_kernel(is_up, where_ref, rate_ref, clip_ref, squares, *refs):
@@ -839,10 +855,10 @@
         shard[:, cs] = low
 
 
-def update(is_up, k, mat, part, where, scalars, gfin, gsib, state, before):
+def update(is_up, k, mat, part, parts, where, scalars, gfin, gsib, state, before):
     rows, cols = state[0].shape[1:]
-    blocks = next(b for b in (5, 4, 2, 1) if rows % (32 * b) == 0)
-    br = rows // (2 * blocks)
+    blocks = next(b for b in (5, 4, 2, 1) if rows % (16 * parts * b) == 0)
+    br = rows // (parts * blocks)
     skip = part * blocks
     dim = gfin.shape[2]
 
@@ -852,7 +868,7 @@
     any_spec = pl.BlockSpec(memory_space=pl.ANY)
     state_spec = pl.BlockSpec((1, br, cols), mine)
     if is_up:
-        g_specs = [pl.BlockSpec((1, br, dim), lambda i, w: (k, w[1] * 2 * blocks + skip + i, 0)), pl.BlockSpec((1, br, dim), lambda i, w: (k // 2, skip + i, 0))]
+        g_specs = [pl.BlockSpec((1, br, dim), lambda i, w: (k, w[1] * parts * blocks + skip + i, 0)), pl.BlockSpec((1, br, dim), lambda i, w: (k // 2, skip + i, 0))]
         g_args = [gfin, gsib]
     else:
         g_specs, g_args = [pl.BlockSpec((1, br, dim), lambda i, w: (k, skip + i, 0))], [gfin]
@@ -863,16 +879,16 @@
     shape = state[0].shape
     return pl.pallas_call(
         functools.partial(update_kernel, int(is_up)),
-        out_shape=[S(shape, F32)] * 3 + [S((2, 4 * rows, cols), BF16), S((rows // 2, cols), BF16)],
+        out_shape=[S(shape, F32)] * 3 + [S((2, 4 * rows, cols), BF16), S((rows // parts, cols), BF16)],
         grid_spec=pltpu.PrefetchScalarGridSpec(
             num_scalar_prefetch=1, grid=(blocks,),
             in_specs=[smem, smem, pl.BlockSpec(memory_space=pltpu.VMEM)] + g_specs + [state_spec] * 3 + [any_spec] * len(held),
             out_specs=[state_spec] * 3 + [
-                pl.BlockSpec((1, br, cols), lambda i, w: (mat, w[0] * 2 * blocks + skip + i, 0)), pl.BlockSpec((br, cols), lambda i, w: (i, 0))],
+                pl.BlockSpec((1, br, cols), lambda i, w: (mat, w[0] * parts * blocks + skip + i, 0)), pl.BlockSpec((br, cols), lambda i, w: (i, 0))],
             scratch_shapes=[pltpu.VMEM((8, 128), F32)],
         ),
         input_output_aliases={n_in + i: i for i in range(len(held))},
-        cost_estimate=pl.CostEstimate(flops=15 * rows * cols, bytes_accessed=16 * rows * cols, transcendentals=rows * cols),
+        cost_estimate=pl.CostEstimate(flops=30 * rows * cols // parts, bytes_accessed=32 * rows * cols // parts, transcendentals=2 * rows * cols // parts),
         name="adam",
     )(where, *scalars, *g_args, *state, *held)
 
@@ -881,7 +897,7 @@
 TO_SIB = [(0, 1), (1, 0), (2, 3), (3, 2)]
 
 
-ORDER = [(up, k, mat, part) for up, k, mat in ((False, 2, 0), (False, 0, 1), (True, 3, 0), (True, 1, 1)) for part in (0, 1)]
+ORDER = [(up, k, mat, part, parts) for up, k, mat, parts in ((False, 2, 0, 4), (False, 0, 1, 2), (True, 3, 0, 2), (True, 1, 1, 4)) for part in range(parts)]
 
 
 def solution(mesh):
@@ -896,9 +912,7 @@
         place = lax.axis_index("data")
         core = place % 2
         side = place // 2
-        where = jnp.stack([place, core]).astype(jnp.int32)
-        act_in, where = lax.optimization_barrier((act_in, where))
-        gfin, gsib, squares = gradients(act_in, grad_out, w_up, w_down)
+        gfin, gsib, squares, where = gradients(act_in, grad_out, w_up, w_down)
         norm_val = jnp.sqrt(jnp.sum(squares))
         scalars = (learn_rate, clip_norm, squares)
         state = {False: (master_down, mom_down, var_down), True: (master_up, mom_up, var_up)}
@@ -914,8 +928,8 @@
             done[is_up][3] = lax.dynamic_update_slice(wide, piece[None], (mat, start, 0))
 
         sent = []
-        for is_up, k, mat, part in ORDER:
-            *done[is_up], shard = update(is_up, k, mat, part, where, scalars, gfin, gsib, state[is_up], done[is_up])
+        for is_up, k, mat, part, parts in ORDER:
+            *done[is_up], shard = update(is_up, k, mat, part, parts, where, scalars, gfin, gsib, state[is_up], done[is_up])
             where, shard = lax.optimization_barrier((where, shard))
             got = lax.ppermute(shard, "data", TO_FAR)
             sent.append((is_up, mat, part, shard, got))

time: 930 us -> 954 us (1.026)
  local copies, waits for them, and re-layouts: 24 us -> 35.1 us
    pallas_call x8 -> x12, Pallas kernels: 65.5 us -> 83.2 us  [update(): pl.pallas_call(functools.partial(update_kernel, int(is_up)), out_shape=[S...]
    dynamic_update_slice x24 -> x36, local copies, waits for them, and re-layouts: 23.9 us -> 35.1 us  [put(): lax.dynamic_update_slice(wide, piece[None], (mat, start, 0))]
    pallas_call x1, Pallas kernels: 736 us -> 725 us  [gradients(): pl.pallas_call(functools.partial(grad_kernel, rows, bm, bz, min(256, dim)...]
    ppermute x8 -> x12, waiting for transfers between devices: 79.1 us -> 78.5 us  [local_step(): got = lax.ppermute(shard, 'data', TO_FAR)]
  transfers between devices with their start and end apart: 24 -> 36, of which waited for: 8 -> 15; matrix products, arithmetic and copies ran while one was open for 3% -> 4% of each run, Pallas kernels for 6% -> 8%
where the time goes in v3:
time: 954 us; the launch traced here: 945 us
  Pallas kernels  808 us (85%)
  waiting for transfers between devices  83.2 us (9%)
  local copies, waits for them, and re-layouts  35.1 us (4%)
  starting transfers between devices  12.8 us (1%)
    pallas_call x1, Pallas kernels, gradients(): pl.pallas_call(functools.partial(grad_kernel, rows, bm, bz, min(256, dim)...  725 us
    pallas_call x12, Pallas kernels, update(): pl.pallas_call(functools.partial(update_kernel, int(is_up)), out_shape=[S...  83.2 us
    ppermute x12, waiting for transfers between devices, local_step(): got = lax.ppermute(shard, 'data', TO_FAR)  78.5 us
    dynamic_update_slice x36, local copies, waits for them, and re-layouts, put(): lax.dynamic_update_slice(wide, piece[None], (mat, start, 0))  35.1 us
  transfers between devices with their start and end apart: 36, of which 15 were waited for; matrix products, arithmetic and copies ran while one was open for 4% of the time, Pallas kernels for 8%

profile of v3, /device:TPU:0, one launch (start us, length us, event | category | flops | bytes accessed | tf_op | source)
XLA Modules:
  0.0 944.5 jit_solution(3930620520642560564)
XLA Ops:
  1.9 725.2 %grads.1 = (f32[4,640,1280]{2,1,0:T(8,128)}, f32[2,320,1280]{2,1,0:T(8,128)}, f32[8,128]{1,0:T(8,128)}, s32[2]{0:T(128)}, bf16[2,1280,2560]{2,1,0:T(8,128)(2,1)}...) custom-call(bf16[8192,1280]{1,0:T(8,128)(2,1)} %x.1, ...), custom_call_target="tpu_custom_call" | custom-call | flops 536870912000 | bytes 1500000000 | tf_op jit(solution)/shard_map/grads/pallas_call | solution.py:812
  727.1 6.2 adam.12
  734.0 6.3 adam.13
  740.4 1.6 collective-permute-start.10
  742.0 6.3 adam.14
  748.5 6.3 adam.15
  754.7 8.2 adam.16
  762.9 8.2 adam.17
  771.1 8.2 adam.18
  779.4 8.2 adam.19
  787.6 6.5 adam.20
  794.0 6.2 adam.21
  800.2 6.2 adam.22
  806.5 6.5 adam.23
  814.8 1.8 bitcast_dynamic-update-slice_fusion.35
  816.7 1.8 bitcast_dynamic-update-slice_fusion.34
  818.5 1.6 collective-permute-start.8
  820.1 1.8 bitcast_dynamic-update-slice_fusion.33
  822.1 1.8 bitcast_dynamic-update-slice_fusion.32
  824.2 0.8 bitcast_dynamic-update-slice_fusion.31
  825.4 1.8 bitcast_dynamic-update-slice_fusion.30
  827.2 0.8 bitcast_dynamic-update-slice_fusion.29
  828.0 1.2 collective-permute-done.16
  829.3 0.8 bitcast_dynamic-update-slice_fusion.28
  830.1 1.6 collective-permute-start.6
  831.7 0.8 bitcast_dynamic-update-slice_fusion.27
  832.5 3.3 collective-permute-done.8
  835.8 0.8 bitcast_dynamic-update-slice_fusion.26
  836.6 1.0 collective-permute-done.18
  837.7 0.8 bitcast_dynamic-update-slice_fusion.25
  838.8 0.9 bitcast_dynamic-update-slice_fusion.11
  839.8 13.6 %collective-permute-done.7 = bf16[320,1280]{1,0:T(8,128)(2,1)S(1)} collective-permute-done((bf16[320,1280]{1,0:T(8,128)(2,1)S(1)}, bf16[320,1280]{1,0:T(8,128)(2,1)S(1)}, u32[]{:S(2)}, u32[]{:S(2)}) %collective-permute-start.7) | collective-permute-done | bytes 819232 | tf_op jit(solution)/shard_map/ppermute | solution.py:934
  853.4 0.9 bitcast_dynamic-update-slice_fusion.10
  854.3 0.8 collective-permute-done.20
  855.2 0.8 bitcast_dynamic-update-slice_fusion.24
  856.4 0.9 bitcast_dynamic-update-slice_fusion.9
  857.3 13.6 %collective-permute-done.6 = bf16[320,1280]{1,0:T(8,128)(2,1)S(1)} collective-permute-done((bf16[320,1280]{1,0:T(8,128)(2,1)S(1)}, bf16[320,1280]{1,0:T(8,128)(2,1)S(1)}, u32[]{:S(2)}, u32[]{:S(2)}) %collective-permute-start.6) | collective-permute-done | bytes 819232 | tf_op jit(solution)/shard_map/ppermute | solution.py:934
  871.4 0.9 bitcast_dynamic-update-slice_fusion.8
  872.4 0.9 bitcast_dynamic-update-slice_fusion.7
  874.2 0.9 bitcast_dynamic-update-slice_fusion.6
  875.1 13.3 %collective-permute-done.5 = bf16[160,2560]{1,0:T(8,128)(2,1)S(1)} collective-permute-done((bf16[160,2560]{1,0:T(8,128)(2,1)S(1)}, bf16[160,2560]{1,0:T(8,128)(2,1)S(1)}, u32[]{:S(2)}, u32[]{:S(2)}) %collective-permute-start.5) | collective-permute-done | bytes 819232 | tf_op jit(solution)/shard_map/ppermute | solution.py:934
  888.5 0.9 bitcast_dynamic-update-slice_fusion.5
  889.9 0.9 bitcast_dynamic-update-slice_fusion.4
  890.9 0.9 bitcast_dynamic-update-slice_fusion.3
  891.9 14.1 %collective-permute-done.4 = bf16[160,2560]{1,0:T(8,128)(2,1)S(1)} collective-permute-done((bf16[160,2560]{1,0:T(8,128)(2,1)S(1)}, bf16[160,2560]{1,0:T(8,128)(2,1)S(1)}, u32[]{:S(2)}, u32[]{:S(2)}) %collective-permute-start.4) | collective-permute-done | bytes 819232 | tf_op jit(solution)/shard_map/ppermute | solution.py:934
  906.4 0.9 bitcast_dynamic-update-slice_fusion.2
  907.3 0.9 bitcast_dynamic-update-slice_fusion.1
  908.8 0.8 bitcast_dynamic-update-slice_fusion.23
  909.6 5.2 collective-permute-done.3
  915.2 0.8 bitcast_dynamic-update-slice_fusion.22
  915.9 0.9 bitcast_dynamic-update-slice_fusion
  916.9 1.7 collective-permute-start
  919.3 4.2 collective-permute-done.2
  923.6 0.8 bitcast_dynamic-update-slice_fusion.20
  924.4 1.0 collective-permute-done.30
  926.2 0.8 bitcast_dynamic-update-slice_fusion.18
  927.0 5.3 collective-permute-done.1
  932.4 0.8 bitcast_dynamic-update-slice_fusion.17
  933.1 0.8 bitcast_dynamic-update-slice_fusion.16
  933.9 0.8 bitcast_dynamic-update-slice_fusion.15
  934.7 5.7 collective-permute-done
  940.4 0.8 bitcast_dynamic-update-slice_fusion.14
  941.2 0.8 bitcast_dynamic-update-slice_fusion.13
  942.2 0.8 bitcast_dynamic-update-slice_fusion.12
  (76 shorter events, 9.3 us)
Async XLA Ops:
  733.4 81.1 %collective-permute-start.12 = (bf16[160,1280]{1,0:T(8,128)(2,1)}, bf16[160,1280]{1,0:T(8,128)(2,1)}, u32[]{:S(2)}, u32[]{:S(2)}) collective-permute-start(bf16[160,1280]{1,0:T(8,128)(2,1)} %get-tuple-element.210), channel_id=1, source_target_pairs={{0,1},{1,0},{2,3},{3,2},{4,5},{5,4},{6,7},{7,6}} | collective-permute-start | bytes 1228808 | tf_op jit(solution)/shard_map/ppermute | solution.py:923
  733.7 83.0 %collective-permute-start.11 = (bf16[160,1280]{1,0:T(8,128)(2,1)}, bf16[160,1280]{1,0:T(8,128)(2,1)}, u32[]{:S(2)}, u32[]{:S(2)}) collective-permute-start(bf16[160,1280]{1,0:T(8,128)(2,1)} %get-tuple-element.210), channel_id=1, source_target_pairs={{0,2},{2,0},{1,3},{3,1},{4,6},{6,4},{5,7},{7,5}} | collective-permute-start | bytes 1228808 | tf_op jit(solution)/shard_map/ppermute | solution.py:934
  740.3 78.2 %collective-permute-start.13 = (bf16[160,1280]{1,0:T(8,128)(2,1)}, bf16[160,1280]{1,0:T(8,128)(2,1)}, u32[]{:S(2)}, u32[]{:S(2)}) collective-permute-start(bf16[160,1280]{1,0:T(8,128)(2,1)} %get-tuple-element.209), channel_id=1, source_target_pairs={{0,1},{1,0},{2,3},{3,2},{4,5},{5,4},{6,7},{7,6}} | collective-permute-start | bytes 1228808 | tf_op jit(solution)/shard_map/ppermute | solution.py:923
  740.4 81.5 %collective-permute-start.10 = (bf16[160,1280]{1,0:T(8,128)(2,1)}, bf16[160,1280]{1,0:T(8,128)(2,1)}, u32[]{:S(2)}, u32[]{:S(2)}) collective-permute-start(bf16[160,1280]{1,0:T(8,128)(2,1)} %get-tuple-element.209), channel_id=1, source_target_pairs={{0,2},{2,0},{1,3},{3,1},{4,6},{6,4},{5,7},{7,5}} | collective-permute-start | bytes 1228808 | tf_op jit(solution)/shard_map/ppermute | solution.py:934
  748.3 76.7 %collective-permute-start.15 = (bf16[160,1280]{1,0:T(8,128)(2,1)}, bf16[160,1280]{1,0:T(8,128)(2,1)}, u32[]{:S(2)}, u32[]{:S(2)}) collective-permute-start(bf16[160,1280]{1,0:T(8,128)(2,1)} %get-tuple-element.208), channel_id=1, source_target_pairs={{0,1},{1,0},{2,3},{3,2},{4,5},{5,4},{6,7},{7,6}} | collective-permute-start | bytes 1228808 | tf_op jit(solution)/shard_map/ppermute | solution.py:923
  806.4 6.5 copy-start
  806.5 17.5 %copy-start.4 = (bf16[320,1280]{1,0:T(8,128)(2,1)S(1)}, bf16[320,1280]{1,0:T(8,128)(2,1)}, u32[]{:S(2)}) copy-start(bf16[320,1280]{1,0:T(8,128)(2,1)} %get-tuple-element.206) | copy-start | bytes 2457604
  806.5 22.7 %copy-start.3 = (bf16[320,1280]{1,0:T(8,128)(2,1)S(1)}, bf16[320,1280]{1,0:T(8,128)(2,1)}, u32[]{:S(2)}) copy-start(bf16[320,1280]{1,0:T(8,128)(2,1)} %get-tuple-element.205) | copy-start | bytes 2457604
  806.5 31.1 %copy-start.2 = (bf16[160,2560]{1,0:T(8,128)(2,1)S(1)}, bf16[160,2560]{1,0:T(8,128)(2,1)}, u32[]{:S(2)}) copy-start(bf16[160,2560]{1,0:T(8,128)(2,1)} %get-tuple-element.204) | copy-start | bytes 2457604
  806.5 48.6 %copy-start.1 = (bf16[160,2560]{1,0:T(8,128)(2,1)S(1)}, bf16[160,2560]{1,0:T(8,128)(2,1)}, u32[]{:S(2)}) copy-start(bf16[160,2560]{1,0:T(8,128)(2,1)} %get-tuple-element.203) | copy-start | bytes 2457604
  814.4 56.5 %copy-start.8 = (bf16[80,2560]{1,0:T(8,128)(2,1)S(1)}, bf16[80,2560]{1,0:T(8,128)(2,1)}, u32[]{:S(2)}) copy-start(bf16[80,2560]{1,0:T(8,128)(2,1)} %get-tuple-element.202) | copy-start | bytes 1228804
  814.4 75.0 %copy-start.7 = (bf16[80,2560]{1,0:T(8,128)(2,1)S(1)}, bf16[80,2560]{1,0:T(8,128)(2,1)}, u32[]{:S(2)}) copy-start(bf16[80,2560]{1,0:T(8,128)(2,1)} %get-tuple-element.201) | copy-start | bytes 1228804
  814.5 12.8 %collective-permute-start.9 = (bf16[160,1280]{1,0:T(8,128)(2,1)}, bf16[160,1280]{1,0:T(8,128)(2,1)S(1)}, u32[]{:S(2)}, u32[]{:S(2)}) collective-permute-start(bf16[160,1280]{1,0:T(8,128)(2,1)} %get-tuple-element.208), channel_id=1, source_target_pairs={{0,2},{2,0},{1,3},{3,1},{4,6},{6,4},{5,7},{7,5}} | collective-permute-start | bytes 1228808 | tf_op jit(solution)/shard_map/ppermute | solution.py:934
  814.8 92.5 %copy-start.6 = (bf16[80,2560]{1,0:T(8,128)(2,1)S(1)}, bf16[80,2560]{1,0:T(8,128)(2,1)}, u32[]{:S(2)}) copy-start(bf16[80,2560]{1,0:T(8,128)(2,1)} %get-tuple-element.200) | copy-start | bytes 1228804
  816.7 13.4 %collective-permute-start.17 = (bf16[160,1280]{1,0:T(8,128)(2,1)}, bf16[160,1280]{1,0:T(8,128)(2,1)S(1)}, u32[]{:S(2)}, u32[]{:S(2)}) collective-permute-start(bf16[160,1280]{1,0:T(8,128)(2,1)} %get-tuple-element.207), channel_id=1, source_target_pairs={{0,1},{1,0},{2,3},{3,2},{4,5},{5,4},{6,7},{7,6}} | collective-permute-start | bytes 1228808 | tf_op jit(solution)/shard_map/ppermute | solution.py:923
  818.5 17.3 %collective-permute-start.8 = (bf16[160,1280]{1,0:T(8,128)(2,1)}, bf16[160,1280]{1,0:T(8,128)(2,1)S(1)}, u32[]{:S(2)}, u32[]{:S(2)}) collective-permute-start(bf16[160,1280]{1,0:T(8,128)(2,1)} %get-tuple-element.207), channel_id=1, source_target_pairs={{0,2},{2,0},{1,3},{3,1},{4,6},{6,4},{5,7},{7,5}} | collective-permute-start | bytes 1228808 | tf_op jit(solution)/shard_map/ppermute | solution.py:934
  821.9 2.0 collective-permute-start.14
  823.9 92.0 %copy-start.5 = (bf16[80,2560]{1,0:T(8,128)(2,1)S(1)}, bf16[80,2560]{1,0:T(8,128)(2,1)}, u32[]{:S(2)}) copy-start(bf16[80,2560]{1,0:T(8,128)(2,1)} %get-tuple-element.199) | copy-start | bytes 1228804
  823.9 14.5 %collective-permute-start.19 = (bf16[320,1280]{1,0:T(8,128)(2,1)S(1)}, bf16[320,1280]{1,0:T(8,128)(2,1)S(1)}, u32[]{:S(2)}, u32[]{:S(2)}) collective-permute-start(bf16[320,1280]{1,0:T(8,128)(2,1)S(1)} %copy-done.4), channel_id=1, source_target_pairs={{0,1},{1,0},{2,3},{3,2},{4,5},{5,4},{6,7},{7,6}} | collective-permute-start | bytes 2457608 | tf_op jit(solution)/shard_map/ppermute | solution.py:923
  825.0 28.3 %collective-permute-start.7 = (bf16[320,1280]{1,0:T(8,128)(2,1)S(1)}, bf16[320,1280]{1,0:T(8,128)(2,1)S(1)}, u32[]{:S(2)}, u32[]{:S(2)}) collective-permute-start(bf16[320,1280]{1,0:T(8,128)(2,1)S(1)} %copy-done.4), channel_id=1, source_target_pairs={{0,2},{2,0},{1,3},{3,1},{4,6},{6,4},{5,7},{7,5}} | collective-permute-start | bytes 2457608 | tf_op jit(solution)/shard_map/ppermute | solution.py:934
  827.2 2.0 collective-permute-start.16
  829.2 26.8 %collective-permute-start.21 = (bf16[320,1280]{1,0:T(8,128)(2,1)S(1)}, bf16[320,1280]{1,0:T(8,128)(2,1)S(1)}, u32[]{:S(2)}, u32[]{:S(2)}) collective-permute-start(bf16[320,1280]{1,0:T(8,128)(2,1)S(1)} %copy-done.3), channel_id=1, source_target_pairs={{0,1},{1,0},{2,3},{3,2},{4,5},{5,4},{6,7},{7,6}} | collective-permute-start | bytes 2457608 | tf_op jit(solution)/shard_map/ppermute | solution.py:923
  830.1 40.8 %collective-permute-start.6 = (bf16[320,1280]{1,0:T(8,128)(2,1)S(1)}, bf16[320,1280]{1,0:T(8,128)(2,1)S(1)}, u32[]{:S(2)}, u32[]{:S(2)}) collective-permute-start(bf16[320,1280]{1,0:T(8,128)(2,1)S(1)} %copy-done.3), channel_id=1, source_target_pairs={{0,2},{2,0},{1,3},{3,1},{4,6},{6,4},{5,7},{7,5}} | collective-permute-start | bytes 2457608 | tf_op jit(solution)/shard_map/ppermute | solution.py:934
  835.8 1.7 collective-permute-start.18
  837.6 33.4 %collective-permute-start.22 = (bf16[160,2560]{1,0:T(8,128)(2,1)S(1)}, bf16[160,2560]{1,0:T(8,128)(2,1)S(1)}, u32[]{:S(2)}, u32[]{:S(2)}) collective-permute-start(bf16[160,2560]{1,0:T(8,128)(2,1)S(1)} %copy-done.2), channel_id=1, source_target_pairs={{0,1},{1,0},{2,3},{3,2},{4,5},{5,4},{6,7},{7,6}} | collective-permute-start | bytes 2457608 | tf_op jit(solution)/shard_map/ppermute | solution.py:923
  838.5 50.0 %collective-permute-start.5 = (bf16[160,2560]{1,0:T(8,128)(2,1)S(1)}, bf16[160,2560]{1,0:T(8,128)(2,1)S(1)}, u32[]{:S(2)}, u32[]{:S(2)}) collective-permute-start(bf16[160,2560]{1,0:T(8,128)(2,1)S(1)} %copy-done.2), channel_id=1, source_target_pairs={{0,2},{2,0},{1,3},{3,1},{4,6},{6,4},{5,7},{7,5}} | collective-permute-start | bytes 2457608 | tf_op jit(solution)/shard_map/ppermute | solution.py:934
  853.4 1.7 collective-permute-start.20
  855.1 34.3 %collective-permute-start.24 = (bf16[160,2560]{1,0:T(8,128)(2,1)S(1)}, bf16[160,2560]{1,0:T(8,128)(2,1)S(1)}, u32[]{:S(2)}, u32[]{:S(2)}) collective-permute-start(bf16[160,2560]{1,0:T(8,128)(2,1)S(1)} %copy-done.1), channel_id=1, source_target_pairs={{0,1},{1,0},{2,3},{3,2},{4,5},{5,4},{6,7},{7,6}} | collective-permute-start | bytes 2457608 | tf_op jit(solution)/shard_map/ppermute | solution.py:923
  856.0 50.0 %collective-permute-start.4 = (bf16[160,2560]{1,0:T(8,128)(2,1)S(1)}, bf16[160,2560]{1,0:T(8,128)(2,1)S(1)}, u32[]{:S(2)}, u32[]{:S(2)}) collective-permute-start(bf16[160,2560]{1,0:T(8,128)(2,1)S(1)} %copy-done.1), channel_id=1, source_target_pairs={{0,2},{2,0},{1,3},{3,1},{4,6},{6,4},{5,7},{7,5}} | collective-permute-start | bytes 2457608 | tf_op jit(solution)/shard_map/ppermute | solution.py:934
  870.9 37.4 %collective-permute-start.27 = (bf16[80,2560]{1,0:T(8,128)(2,1)S(1)}, bf16[80,2560]{1,0:T(8,128)(2,1)S(1)}, u32[]{:S(2)}, u32[]{:S(2)}) collective-permute-start(bf16[80,2560]{1,0:T(8,128)(2,1)S(1)} %copy-done.8), channel_id=1, source_target_pairs={{0,1},{1,0},{2,3},{3,2},{4,5},{5,4},{6,7},{7,6}} | collective-permute-start | bytes 1228808 | tf_op jit(solution)/shard_map/ppermute | solution.py:923
  870.9 2.9 collective-permute-start.23
  873.8 41.0 %collective-permute-start.3 = (bf16[80,2560]{1,0:T(8,128)(2,1)S(1)}, bf16[80,2560]{1,0:T(8,128)(2,1)S(1)}, u32[]{:S(2)}, u32[]{:S(2)}) collective-permute-start(bf16[80,2560]{1,0:T(8,128)(2,1)S(1)} %copy-done.8), channel_id=1, source_target_pairs={{0,2},{2,0},{1,3},{3,1},{4,6},{6,4},{5,7},{7,5}} | collective-permute-start | bytes 1228808 | tf_op jit(solution)/shard_map/ppermute | solution.py:934
  888.5 2.4 collective-permute-start.25
  889.4 27.5 %collective-permute-start.29 = (bf16[80,2560]{1,0:T(8,128)(2,1)S(1)}, bf16[80,2560]{1,0:T(8,128)(2,1)S(1)}, u32[]{:S(2)}, u32[]{:S(2)}) collective-permute-start(bf16[80,2560]{1,0:T(8,128)(2,1)S(1)} %copy-done.7), channel_id=1, source_target_pairs={{0,1},{1,0},{2,3},{3,2},{4,5},{5,4},{6,7},{7,6}} | collective-permute-start | bytes 1228808 | tf_op jit(solution)/shard_map/ppermute | solution.py:923
  890.9 16.4 %collective-permute-start.26 = (bf16[160,2560]{1,0:T(8,128)(2,1)S(1)}, bf16[160,2560]{1,0:T(8,128)(2,1)S(1)}, u32[]{:S(2)}, u32[]{:S(2)}) collective-permute-start(bf16[160,2560]{1,0:T(8,128)(2,1)S(1)} %collective-permute-done.5), channel_id=1, source_target_pairs={{0,1},{1,0},{2,3},{3,2},{4,5},{5,4},{6,7},{7,6}} | collective-permute-start | bytes 2457608 | tf_op jit(solution)/shard_map/ppermute | solution.py:923
  906.0 17.6 %collective-permute-start.2 = (bf16[80,2560]{1,0:T(8,128)(2,1)S(1)}, bf16[80,2560]{1,0:T(8,128)(2,1)S(1)}, u32[]{:S(2)}, u32[]{:S(2)}) collective-permute-start(bf16[80,2560]{1,0:T(8,128)(2,1)S(1)} %copy-done.7), channel_id=1, source_target_pairs={{0,2},{2,0},{1,3},{3,1},{4,6},{6,4},{5,7},{7,5}} | collective-permute-start | bytes 1228808 | tf_op jit(solution)/shard_map/ppermute | solution.py:934
  907.3 18.9 %collective-permute-start.31 = (bf16[80,2560]{1,0:T(8,128)(2,1)S(1)}, bf16[80,2560]{1,0:T(8,128)(2,1)S(1)}, u32[]{:S(2)}, u32[]{:S(2)}) collective-permute-start(bf16[80,2560]{1,0:T(8,128)(2,1)S(1)} %copy-done.6), channel_id=1, source_target_pairs={{0,1},{1,0},{2,3},{3,2},{4,5},{5,4},{6,7},{7,6}} | collective-permute-start | bytes 1228808 | tf_op jit(solution)/shard_map/ppermute | solution.py:923
  908.3 7.7 collective-permute-start.28
  914.8 17.6 %collective-permute-start.1 = (bf16[80,2560]{1,0:T(8,128)(2,1)S(1)}, bf16[80,2560]{1,0:T(8,128)(2,1)S(1)}, u32[]{:S(2)}, u32[]{:S(2)}) collective-permute-start(bf16[80,2560]{1,0:T(8,128)(2,1)S(1)} %copy-done.6), channel_id=1, source_target_pairs={{0,2},{2,0},{1,3},{3,1},{4,6},{6,4},{5,7},{7,5}} | collective-permute-start | bytes 1228808 | tf_op jit(solution)/shard_map/ppermute | solution.py:934
  915.9 18.0 %collective-permute-start.33 = (bf16[80,2560]{1,0:T(8,128)(2,1)S(1)}, bf16[80,2560]{1,0:T(8,128)(2,1)S(1)}, u32[]{:S(2)}, u32[]{:S(2)}) collective-permute-start(bf16[80,2560]{1,0:T(8,128)(2,1)S(1)} %copy-done.5), channel_id=1, source_target_pairs={{0,1},{1,0},{2,3},{3,2},{4,5},{5,4},{6,7},{7,6}} | collective-permute-start | bytes 1228808 | tf_op jit(solution)/shard_map/ppermute | solution.py:923
  916.9 23.5 %collective-permute-start = (bf16[80,2560]{1,0:T(8,128)(2,1)S(1)}, bf16[80,2560]{1,0:T(8,128)(2,1)S(1)}, u32[]{:S(2)}, u32[]{:S(2)}) collective-permute-start(bf16[80,2560]{1,0:T(8,128)(2,1)S(1)} %copy-done.5), channel_id=1, source_target_pairs={{0,2},{2,0},{1,3},{3,1},{4,6},{6,4},{5,7},{7,5}} | collective-permute-start | bytes 1228808 | tf_op jit(solution)/shard_map/ppermute | solution.py:934
  923.6 1.7 collective-permute-start.30
  925.3 7.8 collective-permute-start.32
  932.4 8.9 collective-permute-start.34
  940.4 1.7 collective-permute-start.35
